TPU v7x, 32 devices: a 4x4x1 block of a 4x4x8 slice. The times are simulated.
32 devices in a mesh: dp: 2 (over z, core), tp: 16 (over x, y).
Axes of the slice: x: 4, y: 4, z: 1, core: 2. Of those that a mesh axis runs over, the one named last changes fastest.
The devices are a block of a 4x4x8 slice.
Arguments:
- x: bfloat16 [5120, 7168], P(('dp', 'tp')), parts along dimension 0
- dy: bfloat16 [5120, 7168], P(('dp', 'tp')), parts along dimension 0
- pre: bfloat16 [5120, 28672], P('dp', 'tp'), parts along dimension 0
- w_in: bfloat16 [7168, 28672], P(None, 'tp')
- w_down: bfloat16 [28672, 7168], P('tp')
Outputs:
- output 1: bfloat16 [5120, 7168], P(('dp', 'tp')), parts along dimension 0
- output 2: bfloat16 [14336, 28672], P('dp', 'tp'), parts along dimension 0
- output 3: bfloat16 [57344, 7168], P(('dp', 'tp')), parts along dimension 0
There are 2 independent parts. A program takes and returns all parts, laid end to end along the dimension named above; an argument that names none is the same for every part.
All inputs are finite; a program needn't handle non-finite values.
Results may differ from a plain program's by a relative error of at most 0.012.
Values are sent between devices in bfloat16 or wider.
A program may use at most 768 MiB of HBM per device.

v0:
```python
import functools
import math

import jax
import jax.numpy as jnp
from jax import lax
from jax.experimental import pallas as pl
from jax.experimental.pallas import tpu as pltpu
from jax.sharding import PartitionSpec as P


MESH = pl.DeviceIdType.MESH
TILE = 256


def act(pre):
    return jax.nn.gelu(pre)


def dw_in_kernel(x_ref, d_pre_ref, dw_down_in, dw_in_ref, dw_down_ref, slab, load_sem, store_sem):
    step, steps = pl.program_id(0), pl.num_programs(0)
    height = slab.shape[1]
    slot = lax.rem(step, 2)

    def load(i, slot):
        rows = pl.ds(pl.multiple_of(i * height, height), height)
        return pltpu.make_async_copy(dw_down_in.at[rows], slab.at[slot], load_sem.at[slot])

    def store(i, slot):
        rows = pl.ds(pl.multiple_of(i * height, height), height)
        return pltpu.make_async_copy(slab.at[slot], dw_down_ref.at[rows], store_sem.at[slot])

    @pl.when(step >= 2)
    def _():
        store(step - 2, slot).wait()

    load(step, slot).start()
    dw_in_ref[...] = lax.dot_general(
        x_ref[...], d_pre_ref[...], (((0,), (0,)), ((), ())), preferred_element_type=jnp.float32
    ).astype(dw_in_ref.dtype)
    load(step, slot).wait()
    store(step, slot).start()

    @pl.when(step == steps - 1)
    def _():
        store(step - 1, 1 - slot).wait()
        store(step, slot).wait()


def dw_in_and_copy(x, d_pre, dw_down, tile):
    tokens, depth = x.shape
    width = d_pre.shape[1]
    steps = depth // tile
    height = dw_down.shape[0] // steps
    assert depth % tile == 0 and steps >= 2 and height * steps == dw_down.shape[0] and height % 16 == 0
    return pl.pallas_call(
        dw_in_kernel,
        grid=(steps,),
        in_specs=[
            pl.BlockSpec((tokens, tile), lambda i: (0, i)),
            pl.BlockSpec((tokens, width), lambda i: (0, 0)),
            pl.BlockSpec(memory_space=pl.ANY),
        ],
        out_specs=[pl.BlockSpec((tile, width), lambda i: (i, 0)), pl.BlockSpec(memory_space=pl.ANY)],
        out_shape=[jax.ShapeDtypeStruct((depth, width), x.dtype), jax.ShapeDtypeStruct(dw_down.shape, x.dtype)],
        scratch_shapes=[
            pltpu.VMEM((2, height, dw_down.shape[1]), x.dtype),
            pltpu.SemaphoreType.DMA((2,)),
            pltpu.SemaphoreType.DMA((2,)),
        ],
        compiler_params=pltpu.CompilerParams(vmem_limit_bytes=60 * 1024 * 1024),
        cost_estimate=pl.CostEstimate(
            flops=2 * tokens * depth * width,
            bytes_accessed=2 * (tokens * depth + tokens * width + 3 * depth * width),
            transcendentals=0,
        ),
    )(x, d_pre, dw_down)


STEPS = ((1, 0), (-1, 0), (0, 1), (0, -1))


def pieces_of(link):
    along_x, up = link < 2, link % 2 == 0
    mine = (0, 1) if along_x else (2, 3)
    other = (2, 3) if along_x else (0, 1)
    if not up:
        mine, other = mine[::-1], other[::-1]
    back = -1 if up else 1

    def at(first, second):
        return (first, second) if along_x else (second, first)

    return (
        [(*at(0, 0), q) for q in mine + other],
        [(*at(back, 0), mine[0])],
        [(*at(0, s), q) for s, order in ((-1, (0, 1)), (1, (1, 0))) for q in (min(other) + order[0], min(other) + order[1])],
        [(*at(0, 2), q) for q in other],
        [(*at(back, s), other[0]) for s in (0, -1, 1, 2)],
    )


class Gather:
    def __init__(self, own, every, send_sem, recv_sem, me, side):
        self.own, self.every, self.send_sem, self.recv_sem = own, every, send_sem, recv_sem
        self.me, self.side, self.rows = me, side, own.shape[0]
        self.unit = self.rows // 4
        self.sent, self.pending = [], {}
        for link, (dx, dy) in enumerate(STEPS):
            flat = [p for stage in pieces_of(link) for p in stage]
            for k, (ox, oy, q) in enumerate(flat):
                key = self.key(ox - dx, oy - dy, q)
                assert key not in self.pending
                self.pending[key] = (link, k)
        self.arrival = dict(self.pending)

    def key(self, ox, oy, q):
        return ox % self.side, oy % self.side, q

    def start_row(self, ox, oy):
        x, y = (lax.rem(m + (o % self.side), self.side) for m, o in zip(self.me, (ox, oy)))
        return pl.multiple_of((x * self.side + y) * self.rows, self.unit)

    def place(self, ox, oy, q):
        return self.every.at[pl.ds(pl.multiple_of(self.start_row(ox, oy) + q * self.unit, 8), self.unit)]

    def copy(self, link, k, source, target):
        dx, dy = STEPS[link]
        x, y = (lax.rem(m + d + self.side, self.side) for m, d in zip(self.me, (dx, dy)))
        return pltpu.make_async_remote_copy(
            src_ref=source,
            dst_ref=target,
            send_sem=self.send_sem.at[link, k],
            recv_sem=self.recv_sem.at[link, k],
            device_id={"tp": x * self.side + y},
            device_id_type=MESH,
        )

    def arriving(self, ox, oy, q):
        found = self.pending.pop(self.key(ox, oy, q), None)
        place = self.place(ox, oy, q)
        return [] if found is None else [self.copy(*found, place, place)]

    def wait(self, ox, oy, q):
        for c in self.arriving(ox, oy, q):
            c.wait_recv()

    def send(self, stage, only=slice(None)):
        for before, copy in self.forwards(stage, only):
            for c in before:
                c.wait_recv()
            copy.start()

    def forwards(self, stage, only=slice(None)):
        copies = []
        todo = [(link, pieces_of(link)) for link in range(4)]
        count = len(todo[0][1][stage])
        for i in range(count)[only]:
            for link, stages in todo:
                k = sum(len(s) for s in stages[:stage]) + i
                ox, oy, q = stages[stage][i]
                place = self.place(ox, oy, q)
                if (ox, oy) == (0, 0):
                    before, source = [], self.own.at[pl.ds(q * self.unit, self.unit)]
                else:
                    before, source = self.arriving(ox, oy, q), place
                copies.append((before, self.copy(link, k, source, place)))
                self.sent.append((link, k, place))
        return copies

    def wait_shard(self, ox, oy):
        for q in range(4):
            self.wait(ox, oy, q)

    def finish(self):
        for key in list(self.pending):
            self.wait(*key)
        for link, k, place in self.sent:
            self.copy(link, k, place, place).wait_send()


UP_DOWN = {"y": (2, 3), "x": (0, 1)}


def blocks_of(axis):
    up, down = UP_DOWN[axis]
    high, low = (0, 1) if axis == "y" else (2, 3)
    return {
        high: [(2, "relay", up), (1, "later", up), (-1, "direct", down), (0, "own", high)],
        low: [(2, "relay", down), (-1, "later", down), (1, "direct", up), (0, "own", low)],
    }


def barrier_with_neighbours(me, side):
    barrier = pltpu.get_barrier_semaphore()
    for dx, dy in STEPS:
        x, y = (lax.rem(m + d + side, side) for m, d in zip(me, (dx, dy)))
        pl.semaphore_signal(barrier, inc=1, device_id={"tp": x * side + y}, device_id_type=MESH)
    pl.semaphore_wait(barrier, len(STEPS))


def run(copies):
    for c in copies:
        c.start()
    for c in copies:
        c.wait()


def gather_kernel(side, x_ref, dy_ref, pre_ref, w_down_ref, w_in_ref, x_all, dy_all, hidden_ref, d_pre_ref, dw_down_ref, *rest):
    relay, direct, direct_last, later, own_terms = (rest[4 * i : 4 * i + 4] for i in range(5))
    (
        weights, stage, dy_buf, pre_buf, hidden_buf, d_pre, narrow, wide, dy_tile,
        x_send, x_recv, dy_send, dy_recv, load_sem, store_sem, stage_sem, block_sem, tile_sem, out_sem,
    ) = rest[20:]
    rows, depth = dy_ref.shape
    width = pre_ref.shape[1]
    quarter = depth // 4
    t = lax.axis_index("tp")
    me = lax.div(t, side), lax.rem(t, side)
    barrier_with_neighbours(me, side)

    dys = Gather(dy_ref, dy_all, dy_send, dy_recv, me, side)
    xs = Gather(x_ref, x_all, x_send, x_recv, me, side)
    dys.send(0)

    def load_quarter(q):
        return pltpu.make_async_copy(w_in_ref.at[pl.ds(q * quarter, quarter)], stage, stage_sem)

    def tile_at(n, size=TILE):
        return pl.ds(n * size if isinstance(n, int) else pl.multiple_of(n * size, size), size)

    load_quarter(0).start()

    @pl.loop(0, width // TILE)
    def _(n):
        run([pltpu.make_async_copy(w_down_ref.at[tile_at(n)], dy_buf.at[pl.ds(0, TILE)], load_sem.at[0])])
        for k in range(4):
            weights[k, :, tile_at(n)] = dy_buf[0:TILE, k * quarter : (k + 1) * quarter].T

    def rows_of(ox, oy):
        x, y = lax.rem(me[0] + ox + side, side), lax.rem(me[1] + oy + side, side)
        return pl.ds(pl.multiple_of((x * side + y) * rows, rows), rows)

    def wrap(offset):
        return offset % side if isinstance(offset, int) else lax.rem(offset + side, side)

    half = [pl.ds(0, rows), pl.ds(rows, rows)]
    stores = []

    def step_hidden(*pair, own=None):
        here = [rows_of(*offset) for offset in pair]
        at = [d_pre.at[wrap(ox), wrap(oy)] for ox, oy in pair]
        run(
            [
                pltpu.make_async_copy(dy_ref if i == own else dy_all.at[here[i]], dy_buf.at[half[i]], load_sem.at[i])
                for i in range(2)
            ]
            + [pltpu.make_async_copy(pre_ref.at[here[i]], pre_buf.at[half[i]], load_sem.at[2 + i]) for i in range(2)]
        )
        flush()

        @pl.loop(0, width // TILE)
        def _(n):
            tile = tile_at(n)
            d_hidden = jnp.dot(
                dy_buf[...], weights[:, :, tile].reshape(depth, TILE), preferred_element_type=jnp.float32
            )
            hidden, back = jax.vjp(act, pre_buf[:, tile].astype(jnp.float32))
            hidden_buf[:, tile] = hidden.astype(hidden_buf.dtype)
            grad = back(d_hidden)[0].astype(d_pre.dtype)
            for i in range(2):
                at[i][:, tile] = grad[i * rows : (i + 1) * rows]

        for i in range(2):
            stores.append(pltpu.make_async_copy(hidden_buf.at[half[i]], hidden_ref.at[here[i]], store_sem.at[i]))
            stores.append(pltpu.make_async_copy(at[i], d_pre_ref.at[here[i]], store_sem.at[2 + i]))
            if i == own:
                stores.append(pltpu.make_async_copy(dy_buf.at[half[i]], dy_all.at[here[i]], store_sem.at[4]))
        for c in stores:
            c.start()

    def flush():
        for c in stores:
            c.wait()
        stores.clear()

    def steps_hidden(pair):
        flush()

        @pl.loop(0, 2)
        def _(k):
            step_hidden(*pair(k))
            flush()

    leaving = {0: [], 1: []}

    def step_dx(axis, q, offset, kind, index):
        exact = kind in ("later", "own")
        buf, which = (wide, 0) if exact else (narrow, 1)
        for c in leaving[which]:
            c.wait()

        @pl.loop(0, quarter // TILE * 2)
        def _(n):
            tile = tile_at(lax.div(n, 2))
            two = pl.ds(lax.rem(n, 2) * (side // 2), side // 2)
            lines = d_pre[two, offset % side] if axis == "y" else d_pre[offset % side, two]
            term = jnp.dot(
                lines.reshape(side // 2 * rows, width), weights[q, :, tile], preferred_element_type=jnp.float32
            )
            buf[two, :, tile] = term.astype(buf.dtype).reshape(side // 2, rows, TILE)

        if kind == "direct":
            cut = [(buf.at[pl.ds(1, side - 1)], direct[index]), (buf.at[0], direct_last[index])]
        else:
            cut = [(buf, {"relay": relay, "later": later, "own": own_terms}[kind][index])]
        leaving[which] = [pltpu.make_async_copy(*c, block_sem.at[which, i]) for i, c in enumerate(cut)]
        for c in leaving[which]:
            c.start()

    dys.send(1)
    dys.send(2)
    for offset in STEPS:
        dys.wait_shard(*offset)
    steps_hidden(lambda k: ((1 - k, k), (k - 1, -k)))
    dys.send(3)
    dys.send(4, slice(0, 3))
    for s in (1, -1):
        for offset in ((1, s), (-1, s)):
            dys.wait_shard(*offset)
        step_hidden((1, s), (-1, s))
        if s == 1:
            dys.send(4, slice(3, 4))
            xs.send(0)
    for offset in ((2, 0), (0, 2)):
        dys.wait_shard(*offset)
    step_hidden((2, 0), (0, 2))
    for offset in ((2, 1), (2, -1), (1, 2), (-1, 2)):
        dys.wait_shard(*offset)
    steps_hidden(lambda k: ((2, 1 - 2 * k), (1 - 2 * k, 2)))
    dys.wait_shard(2, 2)
    step_hidden((0, 0), (2, 2), own=0)
    xs.send(1)
    xs.send(2)
    flush()
    own = dy_buf.at[half[0]]
    run([pltpu.make_async_copy(x_ref, own, load_sem.at[0])])
    stores.append(pltpu.make_async_copy(own, x_all.at[rows_of(0, 0)], store_sem.at[0]))
    stores[-1].start()
    tiles = dy_tile.shape[-1]

    def load_tile(n, slot):
        return pltpu.make_async_copy(dy_all.at[:, tile_at(n, tiles)], dy_tile.at[slot], tile_sem.at[slot])

    def store_tile(n, slot):
        return pltpu.make_async_copy(stage.at[:, tile_at(slot, tiles)], dw_down_ref.at[:, tile_at(n, tiles)], out_sem.at[slot])

    spare = side * side * rows - quarter
    hidden_loads = [
        pltpu.make_async_copy(hidden_ref.at[pl.ds(0, quarter)], weights.at[0], load_sem.at[1]),
        pltpu.make_async_copy(hidden_ref.at[pl.ds(quarter, spare)], weights.at[1, pl.ds(0, spare)], load_sem.at[2]),
    ]
    for axis in ("y", "x"):
        for q, blocks in blocks_of(axis).items():
            load_quarter(q).wait()

            @pl.loop(0, quarter // TILE)
            def _(n):
                weights[q, :, tile_at(n)] = stage[tile_at(n), :].T

            if q < 3:
                load_quarter(q + 1).start()
            else:
                for c in hidden_loads + [load_tile(0, 0)]:
                    c.start()
            for offset, kind, index in blocks:
                step_dx(axis, q, offset, kind, index)
            if q == 1:
                xs.send(3)
    xs.send(4, slice(0, 3))
    for c in hidden_loads:
        c.wait()
    count = depth // tiles
    final = xs.forwards(4, slice(3, 4))

    @pl.loop(0, count)
    def _(n):
        slot = lax.rem(n, 2)

        @pl.when(n == 4)
        def _():
            for before, copy in final:
                for c in before:
                    c.wait_recv()
                copy.start()

        @pl.when(n + 1 < count)
        def _():
            load_tile(n + 1, 1 - slot).start()

        @pl.when(n >= 2)
        def _():
            store_tile(n - 2, slot).wait()

        load_tile(n, slot).wait()
        hidden = jnp.concatenate([weights[0], weights[1, 0:spare, :]], axis=0)
        stage[:, tile_at(slot, tiles)] = lax.dot_general(
            hidden, dy_tile[slot], (((0,), (0,)), ((), ())), preferred_element_type=jnp.float32
        ).astype(stage.dtype)
        store_tile(n, slot).start()

    for c in stores + leaving[0] + leaving[1]:
        c.wait()
    for n in (count - 2, count - 1):
        store_tile(n, n % 2).wait()
    dys.finish()
    xs.finish()


def gather_and_differentiate(x, dy, pre, w_down, w_in, group):
    side = math.isqrt(group)
    assert side == 4 and side * side == group
    rows, depth = dy.shape
    width = pre.shape[1]
    quarter, tile = depth // 4, 2 * TILE
    assert rows % 32 == 0 and width % TILE == 0 and quarter % TILE == 0 and depth // tile > 4
    assert quarter < group * rows <= 2 * quarter and width == quarter
    like = jax.ShapeDtypeStruct
    any_space = pl.BlockSpec(memory_space=pl.ANY)
    block = (side, rows, quarter)
    dma = pltpu.SemaphoreType.DMA
    outs = pl.pallas_call(
        functools.partial(gather_kernel, side),
        out_shape=[like((group * rows, depth), x.dtype)] * 2
        + [like((group * rows, width), x.dtype)] * 2
        + [like((width, depth), x.dtype)]
        + [like(block, x.dtype)] * 4
        + [like((side - 1, *block[1:]), x.dtype)] * 4
        + [like(block[1:], x.dtype)] * 4
        + [like(block, jnp.float32)] * 8,
        in_specs=[any_space] * 5,
        out_specs=[any_space] * 25,
        scratch_shapes=[
            pltpu.VMEM((4, quarter, width), x.dtype),
            pltpu.VMEM((quarter, width), x.dtype),
            pltpu.VMEM((2 * rows, depth), x.dtype),
            pltpu.VMEM((2 * rows, width), x.dtype),
            pltpu.VMEM((2 * rows, width), x.dtype),
            pltpu.VMEM((side, side, rows, width), x.dtype),
            pltpu.VMEM(block, x.dtype),
            pltpu.VMEM(block, jnp.float32),
            pltpu.VMEM((2, group * rows, tile), x.dtype),
            *[dma((4, 15))] * 4,
            dma((4,)),
            dma((5,)),
            dma,
            dma((2, 2)),
            dma((2,)),
            dma((2,)),
        ],
        compiler_params=pltpu.CompilerParams(
            collective_id=0, has_side_effects=True, vmem_limit_bytes=67_043_328
        ),
        cost_estimate=pl.CostEstimate(
            flops=6 * group * rows * depth * width,
            bytes_accessed=2 * (group * rows * (7 * depth + 4 * width) + 3 * depth * width),
            transcendentals=0,
        ),
        name="gather_and_differentiate",
    )(x, dy, pre, w_down, w_in)
    return *outs[:5], *(outs[5 + 4 * i : 9 + 4 * i] for i in range(5))


def shift(value, link, side):
    dx, dy = STEPS[link]
    target = lambda x, y: (x + dx) % side * side + (y + dy) % side
    return lax.ppermute(value, "tp", [(x * side + y, target(x, y)) for x in range(side) for y in range(side)])


def scatter_kernel(side, *refs):
    relay, direct, direct_last, later, own_terms = (refs[4 * i : 4 * i + 4] for i in range(5))
    (
        dx_ref, later_got, last_got, cross_got, later_out, cross_out, exact_in, narrow_in, sums, dx_buf,
        later_send, later_recv, last_send, last_recv, cross_send, cross_recv, exact_sem, narrow_sem, dx_sem,
    ) = refs[20:]
    rows, quarter = dx_buf.shape[1:]
    t = lax.axis_index("tp")
    me = lax.div(t, side), lax.rem(t, side)
    barrier_with_neighbours(me, side)

    def remote(link, source, target, send_sem, recv_sem):
        dx, dy = STEPS[link]
        x, y = (lax.rem(m + d + side, side) for m, d in zip(me, (dx, dy)))
        return pltpu.make_async_remote_copy(
            src_ref=source,
            dst_ref=target,
            send_sem=send_sem,
            recv_sem=recv_sem,
            device_id={"tp": x * side + y},
            device_id_type=MESH,
        )

    last_copies = [
        remote(link, direct_last[link], last_got.at[link], last_send.at[link], last_recv.at[link]) for link in range(4)
    ]
    later_copies = {
        (link, j): remote(link, later_out.at[link, j], later_got.at[link, j], later_send.at[link, j], later_recv.at[link, j])
        for link in range(4)
        for j in range(side)
    }
    for c in last_copies:
        c.start()

    takes = {}
    for axis, other in (("y", "x"), ("x", "y")):
        (up, down), (cross_up, cross_down) = UP_DOWN[axis], UP_DOWN[other]
        high, low = (0, 1) if axis == "y" else (2, 3)
        takes[high] = up, down, cross_up, cross_down
        takes[low] = down, up, cross_down, cross_up
    step = lambda link: 1 if link in (0, 2) else side - 1
    cross_copies = {
        (q, k): remote(
            takes[q][3 if k == 1 else 2], cross_out.at[q, k], cross_got.at[q, k], cross_send.at[q, k], cross_recv.at[q, k]
        )
        for q in range(4)
        for k in range(3)
    }

    def add(target, *parts):
        strip = 16

        @pl.loop(0, rows // strip)
        def _(i):
            at = pl.ds(pl.multiple_of(i * strip, strip), strip)
            total = parts[0][at, :].astype(jnp.float32)
            for part in parts[1:]:
                total = total + part[at, :].astype(jnp.float32)
            target[at, :] = total.astype(target.dtype)

    order = [2, 1, side - 1, 0]
    tasks = [("later", link, j, later[link].at[j], relay[link].at[j]) for j in order for link in range(4)]
    for j in order:
        for q in range(4):
            link = takes[q][1]
            tasks.append(("sum", q, j, own_terms[q].at[j], None if j == 0 else direct[link].at[j - 1]))
    slots = exact_in.shape[0]

    def loads(n):
        _, _, _, exact, narrow = tasks[n]
        slot = n % slots
        copies = [pltpu.make_async_copy(exact, exact_in.at[slot], exact_sem.at[slot])]
        if narrow is not None:
            copies.append(pltpu.make_async_copy(narrow, narrow_in.at[slot], narrow_sem.at[slot]))
        return copies

    for n in range(slots - 1):
        for c in loads(n):
            c.start()
    for n, (kind, which, j, _, narrow) in enumerate(tasks):
        if n + slots - 1 < len(tasks):
            for c in loads(n + slots - 1):
                c.start()
        for c in loads(n):
            c.wait()
        exact, slot = exact_in.at[n % slots], n % slots
        if kind == "later":
            add(later_out.at[which, j], exact, narrow_in.at[slot])
            later_copies[which, j].start()
            continue
        q = which
        main, side_link, _, near_link = takes[q]
        later_copies[main, j].wait_recv()
        if narrow is None:
            last_copies[side_link].wait_recv()
            arrived = last_got.at[side_link]
        else:
            arrived = narrow_in.at[slot]
        parts = exact, later_got.at[main, j], arrived
        if j == 2:
            add(cross_out.at[q, 0], *parts)
            cross_copies[q, 0].start()
        elif j == step(near_link):
            add(cross_out.at[q, 1], *parts)
            cross_copies[q, 1].start()
        else:
            add(sums.at[q, 0 if j == 0 else 1], *parts)
    for q in range(4):
        cross_copies[q, 0].wait_recv()
        add(cross_out.at[q, 2], sums.at[q, 1], cross_got.at[q, 0])
        cross_copies[q, 2].start()
    outs = []
    for q in range(4):
        cross_copies[q, 1].wait_recv()
        cross_copies[q, 2].wait_recv()
        add(dx_buf.at[q], sums.at[q, 0], cross_got.at[q, 2], cross_got.at[q, 1])
        outs.append(pltpu.make_async_copy(dx_buf.at[q], dx_ref.at[:, pl.ds(q * quarter, quarter)], dx_sem.at[q]))
        outs[-1].start()
    for c in outs:
        c.wait()
    for c in [*last_copies, *later_copies.values(), *cross_copies.values()]:
        c.wait_send()


def finish_scatter(relay, direct, direct_last, later, own_terms):
    side, rows, quarter = relay[0].shape
    kind = relay[0].dtype
    any_space = pl.BlockSpec(memory_space=pl.ANY)
    dma = pltpu.SemaphoreType.DMA
    piece, slots = (rows, quarter), 4
    return pl.pallas_call(
        functools.partial(scatter_kernel, side),
        out_shape=jax.ShapeDtypeStruct((rows, 4 * quarter), kind),
        in_specs=[any_space] * 20,
        out_specs=any_space,
        scratch_shapes=[
            pltpu.VMEM((4, side, *piece), kind),
            pltpu.VMEM((4, *piece), kind),
            pltpu.VMEM((4, 3, *piece), kind),
            pltpu.VMEM((4, side, *piece), kind),
            pltpu.VMEM((4, 3, *piece), kind),
            pltpu.VMEM((slots, *piece), jnp.float32),
            pltpu.VMEM((slots, *piece), kind),
            pltpu.VMEM((4, 2, *piece), jnp.float32),
            pltpu.VMEM((4, *piece), kind),
            dma((4, side)),
            dma((4, side)),
            dma((4,)),
            dma((4,)),
            dma((4, 3)),
            dma((4, 3)),
            dma((slots,)),
            dma((slots,)),
            dma((4,)),
        ],
        compiler_params=pltpu.CompilerParams(
            collective_id=1, has_side_effects=True, vmem_limit_bytes=67_043_328
        ),
        cost_estimate=pl.CostEstimate(
            flops=8 * side * rows * quarter, bytes_accessed=60 * side * rows * quarter, transcendentals=0
        ),
        name="finish_scatter",
    )(*relay, *direct, *direct_last, *later, *own_terms)


def solution(mesh):
    group = mesh.shape["tp"]
    side = math.isqrt(group)

    def step(x, dy, pre, w_in, w_down):
        x_all, _, _, d_pre, dw_down, relay, direct, direct_last, later, own_terms = gather_and_differentiate(
            x, dy, pre, w_down, w_in, group
        )
        relay = [shift(block, link, side) for link, block in enumerate(relay)]
        direct = [shift(block, link, side) for link, block in enumerate(direct)]
        dw_in, dw_down = dw_in_and_copy(x_all, d_pre, dw_down, 2 * TILE)
        dw_in, dw_down, later = lax.optimization_barrier((dw_in, dw_down, later))
        dx = finish_scatter(relay, direct, direct_last, later, own_terms)
        return dx, dw_in, dw_down

    tokens = P(("dp", "tp"), None)
    step = jax.shard_map(
        step,
        mesh=mesh,
        in_specs=(tokens, tokens, P("dp", "tp"), P(None, "tp"), P("tp", None)),
        out_specs=(tokens, P("dp", "tp"), tokens),
        check_vma=False,
    )
    return step
```

profile of v0, /device:TPU:97, one launch (start us, length us, event | category | flops | bytes accessed | tf_op | source)
XLA Modules:
  0.0 632.7 jit_solution(15368927649473540094)
XLA Ops:
  0.6 413.7 %gather_and_differentiate.1 = (bf16[2560,7168]{1,0:T(8,128)(2,1)}, bf16[2560,7168]{1,0:T(8,128)(2,1)}, bf16[2560,1792]{1,0:T(8,128)(2,1)}, bf16[2560,1792]{1,0:T...) custom-call(bf16[160,7168]{1,0:T(8,128)(2,1)} %x_ref.1, ...), custom_call_target="tpu_custom_call" | custom-call | flops 197300060160 | bytes 370671616 | tf_op jit(solution)/shard_map/gather_and_differentiate/pallas_call | solution.py:432
  414.3 0.1 collective-permute-start.4
  414.5 2.6 collective-permute-start.5
  417.1 0.0 collective-permute-start.6
  417.1 2.7 collective-permute-start.7
  419.8 0.0 collective-permute-start
  419.8 32.8 %collective-permute-done.4.refs_4_ = bf16[3,160,1792]{2,1,0:T(8,128)(2,1)} collective-permute-done((bf16[3,160,1792]{2,1,0:T(8,128)(2,1)}, bf16[3,160,1792]{2,1,0:T(8,128)(2,1)}, u32[]{:S(2)}, u32[]{:S(2)}) %collective-permute-start.4) | collective-permute-done | bytes 1720352 | tf_op jit(solution)/shard_map/ppermute | solution.py:477
  452.6 0.0 collective-permute-start.1
  452.6 0.0 collective-permute-done.5.refs_5_
  452.6 0.3 collective-permute-start.2
  452.9 1.8 collective-permute-done.6.refs_6_
  454.7 0.6 collective-permute-start.3
  455.2 76.6 %shard_map.76 = (bf16[7168,1792]{1,0:T(8,128)(2,1)}, bf16[1792,7168]{1,0:T(8,128)(2,1)}) custom-call(bf16[2560,7168]{1,0:T(8,128)(2,1)} %get-tuple-element.46.x_ref, bf16[2560,1792]{1,0:T(8,128)(2,1)} %get-tuple-element.47.d_pre_ref, bf16[1792,7168]{1,0:T(8,128)(2,1)} %get-tuple-element.48.dw_down_in), custom_call_target="tpu_custom_call" | custom-call | flops 65766686720 | bytes 122945536 | tf_op jit(solution)/shard_map/pallas_call | solution.py:56
  531.8 0.0 collective-permute-done.7.refs_7_
  531.8 0.0 collective-permute-done.refs_0_
  531.8 0.0 collective-permute-done.1.refs_1_
  531.8 0.0 collective-permute-done.2.refs_2_
  531.9 0.0 collective-permute-done.3.refs_3_
  531.9 97.7 %finish_scatter.1 = bf16[160,7168]{1,0:T(8,128)(2,1)} custom-call(bf16[4,160,1792]{2,1,0:T(8,128)(2,1)} %collective-permute-done.refs_0_, bf16[4,160,1792]{2,1,0:T(8,128)(2,1)} %collective-permute-done.1.refs_1_, bf16[4,160,1792]{2,1,0:T(8,128)(2,1)} %collective-permute-done.2.refs_2_, bf16[4,160,1792]{2,1,0:T(8,128)(2,1)} %collective-permute-done.3.refs_3_, ...), custom_call_target="tpu_custom_call" | custom-call | flops 9175040 | bytes 68812800 | tf_op jit(solution)/shard_map/finish_scatter/pallas_call | solution.py:610
  629.5 3.2 copy.9
Async XLA Ops:
  414.3 38.2 %collective-permute-start.4 = (bf16[3,160,1792]{2,1,0:T(8,128)(2,1)}, bf16[3,160,1792]{2,1,0:T(8,128)(2,1)}, u32[]{:S(2)}, u32[]{:S(2)}) collective-permute-start(bf16[3,160,1792]{2,1,0:T(8,128)(2,1)} %get-tuple-element.38), channel_id=1, source_target_pairs={{0,4},{1,5},{2,6},{3,7},{4,8},{5,9},{6,10},{7,11},{8,12},{9,13},{1... | collective-permute-start | bytes 5160968 | tf_op jit(solution)/shard_map/ppermute | solution.py:477
  414.5 38.1 %collective-permute-start.5 = (bf16[3,160,1792]{2,1,0:T(8,128)(2,1)}, bf16[3,160,1792]{2,1,0:T(8,128)(2,1)}, u32[]{:S(2)}, u32[]{:S(2)}) collective-permute-start(bf16[3,160,1792]{2,1,0:T(8,128)(2,1)} %get-tuple-element.39), channel_id=1, source_target_pairs={{0,12},{1,13},{2,14},{3,15},{4,0},{5,1},{6,2},{7,3},{8,4},{9,5},{1... | collective-permute-start | bytes 5160968 | tf_op jit(solution)/shard_map/ppermute | solution.py:477
  417.1 37.6 %collective-permute-start.6 = (bf16[3,160,1792]{2,1,0:T(8,128)(2,1)}, bf16[3,160,1792]{2,1,0:T(8,128)(2,1)}, u32[]{:S(2)}, u32[]{:S(2)}) collective-permute-start(bf16[3,160,1792]{2,1,0:T(8,128)(2,1)} %get-tuple-element.40), channel_id=1, source_target_pairs={{0,1},{1,2},{2,3},{3,0},{4,5},{5,6},{6,7},{7,4},{8,9},{9,10},{10,1... | collective-permute-start | bytes 5160968 | tf_op jit(solution)/shard_map/ppermute | solution.py:477
  417.1 114.7 %collective-permute-start.7 = (bf16[3,160,1792]{2,1,0:T(8,128)(2,1)}, bf16[3,160,1792]{2,1,0:T(8,128)(2,1)}, u32[]{:S(2)}, u32[]{:S(2)}) collective-permute-start(bf16[3,160,1792]{2,1,0:T(8,128)(2,1)} %get-tuple-element.41), channel_id=1, source_target_pairs={{0,3},{1,0},{2,1},{3,2},{4,7},{5,4},{6,5},{7,6},{8,11},{9,8},{10,9... | collective-permute-start | bytes 5160968 | tf_op jit(solution)/shard_map/ppermute | solution.py:477
  419.8 112.0 %collective-permute-start = (bf16[4,160,1792]{2,1,0:T(8,128)(2,1)}, bf16[4,160,1792]{2,1,0:T(8,128)(2,1)}, u32[]{:S(2)}, u32[]{:S(2)}) collective-permute-start(bf16[4,160,1792]{2,1,0:T(8,128)(2,1)} %get-tuple-element.34), channel_id=1, source_target_pairs={{0,4},{1,5},{2,6},{3,7},{4,8},{5,9},{6,10},{7,11},{8,12},{9,13},{1... | collective-permute-start | bytes 6881288 | tf_op jit(solution)/shard_map/ppermute | solution.py:477
  452.6 79.3 %collective-permute-start.1 = (bf16[4,160,1792]{2,1,0:T(8,128)(2,1)}, bf16[4,160,1792]{2,1,0:T(8,128)(2,1)}, u32[]{:S(2)}, u32[]{:S(2)}) collective-permute-start(bf16[4,160,1792]{2,1,0:T(8,128)(2,1)} %get-tuple-element.35), channel_id=1, source_target_pairs={{0,12},{1,13},{2,14},{3,15},{4,0},{5,1},{6,2},{7,3},{8,4},{9,5},{1... | collective-permute-start | bytes 6881288 | tf_op jit(solution)/shard_map/ppermute | solution.py:477
  452.6 79.3 %collective-permute-start.2 = (bf16[4,160,1792]{2,1,0:T(8,128)(2,1)}, bf16[4,160,1792]{2,1,0:T(8,128)(2,1)}, u32[]{:S(2)}, u32[]{:S(2)}) collective-permute-start(bf16[4,160,1792]{2,1,0:T(8,128)(2,1)} %get-tuple-element.36), channel_id=1, source_target_pairs={{0,1},{1,2},{2,3},{3,0},{4,5},{5,6},{6,7},{7,4},{8,9},{9,10},{10,1... | collective-permute-start | bytes 6881288 | tf_op jit(solution)/shard_map/ppermute | solution.py:477
  454.7 77.2 %collective-permute-start.3 = (bf16[4,160,1792]{2,1,0:T(8,128)(2,1)}, bf16[4,160,1792]{2,1,0:T(8,128)(2,1)}, u32[]{:S(2)}, u32[]{:S(2)}) collective-permute-start(bf16[4,160,1792]{2,1,0:T(8,128)(2,1)} %get-tuple-element.37), channel_id=1, source_target_pairs={{0,3},{1,0},{2,1},{3,2},{4,7},{5,4},{6,5},{7,6},{8,11},{9,8},{10,9... | collective-permute-start | bytes 6881288 | tf_op jit(solution)/shard_map/ppermute | solution.py:477
where the time goes:
time: 639 us; the launch traced here: 633 us
  Pallas kernels  588 us (92%)
  waiting for transfers between devices  34.6 us (5%)
    pallas_call x1, Pallas kernels, gather_and_differentiate(): pl.pallas_call(functools.partial(gather_kernel, side), out_shape=[like((g...  414 us
    pallas_call x1, Pallas kernels, finish_scatter(): pl.pallas_call(functools.partial(scatter_kernel, side), out_shape=jax.Sha...  97.7 us
    pallas_call x1, Pallas kernels, dw_in_and_copy(): pl.pallas_call(dw_in_kernel, grid=(steps,), in_specs=[pl.BlockSpec((token...  76.6 us
    ppermute x8, waiting for transfers between devices, shift(): lax.ppermute(value, 'tp', [(x * side + y, target(x, y)) for x in range(si...  34.6 us
  transfers between devices with their start and end apart: 8, of which 2 were waited for; matrix products, arithmetic and copies ran while one was open for 0% of the time, Pallas kernels for 12%

commit v1 on v0

--- a/solution.py
+++ b/solution.py
@@ -250,28 +250,30 @@
     def step_hidden(*pair, own=None):
         here = [rows_of(*offset) for offset in pair]
         at = [d_pre.at[wrap(ox), wrap(oy)] for ox, oy in pair]
+        count = range(len(pair))
         run(
             [
                 pltpu.make_async_copy(dy_ref if i == own else dy_all.at[here[i]], dy_buf.at[half[i]], load_sem.at[i])
-                for i in range(2)
+                for i in count
             ]
-            + [pltpu.make_async_copy(pre_ref.at[here[i]], pre_buf.at[half[i]], load_sem.at[2 + i]) for i in range(2)]
+            + [pltpu.make_async_copy(pre_ref.at[here[i]], pre_buf.at[half[i]], load_sem.at[2 + i]) for i in count]
         )
         flush()
+        used = slice(0, len(pair) * rows)
 
         @pl.loop(0, width // TILE)
         def _(n):
             tile = tile_at(n)
             d_hidden = jnp.dot(
-                dy_buf[...], weights[:, :, tile].reshape(depth, TILE), preferred_element_type=jnp.float32
+                dy_buf[used, :], weights[:, :, tile].reshape(depth, TILE), preferred_element_type=jnp.float32
             )
-            hidden, back = jax.vjp(act, pre_buf[:, tile].astype(jnp.float32))
-            hidden_buf[:, tile] = hidden.astype(hidden_buf.dtype)
+            hidden, back = jax.vjp(act, pre_buf[used, tile].astype(jnp.float32))
+            hidden_buf[used, tile] = hidden.astype(hidden_buf.dtype)
             grad = back(d_hidden)[0].astype(d_pre.dtype)
-            for i in range(2):
+            for i in count:
                 at[i][:, tile] = grad[i * rows : (i + 1) * rows]
 
-        for i in range(2):
+        for i in count:
             stores.append(pltpu.make_async_copy(hidden_buf.at[half[i]], hidden_ref.at[here[i]], store_sem.at[i]))
             stores.append(pltpu.make_async_copy(at[i], d_pre_ref.at[here[i]], store_sem.at[2 + i]))
             if i == own:
@@ -300,15 +302,12 @@
         for c in leaving[which]:
             c.wait()
 
-        @pl.loop(0, quarter // TILE * 2)
+        @pl.loop(0, quarter // TILE)
         def _(n):
-            tile = tile_at(lax.div(n, 2))
-            two = pl.ds(lax.rem(n, 2) * (side // 2), side // 2)
-            lines = d_pre[two, offset % side] if axis == "y" else d_pre[offset % side, two]
-            term = jnp.dot(
-                lines.reshape(side // 2 * rows, width), weights[q, :, tile], preferred_element_type=jnp.float32
-            )
-            buf[two, :, tile] = term.astype(buf.dtype).reshape(side // 2, rows, TILE)
+            tile = tile_at(n)
+            lines = d_pre[:, offset % side] if axis == "y" else d_pre[offset % side]
+            term = jnp.dot(lines.reshape(side * rows, width), weights[q, :, tile], preferred_element_type=jnp.float32)
+            buf[:, :, tile] = term.astype(buf.dtype).reshape(side, rows, TILE)
 
         if kind == "direct":
             cut = [(buf.at[pl.ds(1, side - 1)], direct[index]), (buf.at[0], direct_last[index])]
@@ -320,6 +319,7 @@
 
     dys.send(1)
     dys.send(2)
+    step_hidden((0, 0), own=0)
     for offset in STEPS:
         dys.wait_shard(*offset)
     steps_hidden(lambda k: ((1 - k, k), (k - 1, -k)))
@@ -332,16 +332,10 @@
         if s == 1:
             dys.send(4, slice(3, 4))
             xs.send(0)
-    for offset in ((2, 0), (0, 2)):
-        dys.wait_shard(*offset)
-    step_hidden((2, 0), (0, 2))
-    for offset in ((2, 1), (2, -1), (1, 2), (-1, 2)):
-        dys.wait_shard(*offset)
-    steps_hidden(lambda k: ((2, 1 - 2 * k), (1 - 2 * k, 2)))
-    dys.wait_shard(2, 2)
-    step_hidden((0, 0), (2, 2), own=0)
-    xs.send(1)
-    xs.send(2)
+    for shards in (((2, 0), (0, 2)), ((2, -1), (-1, 2)), ((2, 1), (1, 2)), ((2, 2),)):
+        for offset in shards:
+            dys.wait_shard(*offset)
+        step_hidden(*shards)
     flush()
     own = dy_buf.at[half[0]]
     run([pltpu.make_async_copy(x_ref, own, load_sem.at[0])])
@@ -375,24 +369,28 @@
                     c.start()
             for offset, kind, index in blocks:
                 step_dx(axis, q, offset, kind, index)
-            if q == 1:
+            if q == 0:
+                xs.send(1)
+                xs.send(2)
+            if q == 2:
                 xs.send(3)
-    xs.send(4, slice(0, 3))
     for c in hidden_loads:
         c.wait()
     count = depth // tiles
-    final = xs.forwards(4, slice(3, 4))
+    forwards = {4: xs.forwards(4, slice(0, 3)), 7: xs.forwards(4, slice(3, 4))}
 
     @pl.loop(0, count)
     def _(n):
         slot = lax.rem(n, 2)
 
-        @pl.when(n == 4)
-        def _():
-            for before, copy in final:
-                for c in before:
-                    c.wait_recv()
-                copy.start()
+        for when, copies in forwards.items():
+
+            @pl.when(n == when)
+            def _():
+                for before, copy in copies:
+                    for c in before:
+                        c.wait_recv()
+                    copy.start()
 
         @pl.when(n + 1 < count)
         def _():
@@ -423,7 +421,7 @@
     rows, depth = dy.shape
     width = pre.shape[1]
     quarter, tile = depth // 4, 2 * TILE
-    assert rows % 32 == 0 and width % TILE == 0 and quarter % TILE == 0 and depth // tile > 4
+    assert rows % 32 == 0 and width % TILE == 0 and quarter % TILE == 0 and depth // tile > 7
     assert quarter < group * rows <= 2 * quarter and width == quarter
     like = jax.ShapeDtypeStruct
     any_space = pl.BlockSpec(memory_space=pl.ANY)

time: 639 us -> 606 us (0.948)
  Pallas kernels: 588 us -> 556 us
    pallas_call x1, Pallas kernels: 414 us -> 380 us  [gather_and_differentiate(): pl.pallas_call(functools.partial(gather_kernel, side), out_shape=[like((g...]
  transfers between devices with their start and end apart: 8 -> 8, of which waited for: 2 -> 2; matrix products, arithmetic and copies ran while one was open for 0% -> 0% of each run, Pallas kernels for 12% -> 13%
where the time goes in v1:
time: 606 us; the launch traced here: 602 us
  Pallas kernels  556 us (92%)
  waiting for transfers between devices  35.7 us (6%)
  starting transfers between devices  6.24 us (1%)
    pallas_call x1, Pallas kernels, gather_and_differentiate(): pl.pallas_call(functools.partial(gather_kernel, side), out_shape=[like((g...  380 us
    pallas_call x1, Pallas kernels, finish_scatter(): pl.pallas_call(functools.partial(scatter_kernel, side), out_shape=jax.Sha...  99.8 us
    pallas_call x1, Pallas kernels, dw_in_and_copy(): pl.pallas_call(dw_in_kernel, grid=(steps,), in_specs=[pl.BlockSpec((token...  76.6 us
    ppermute x8, waiting for transfers between devices, shift(): lax.ppermute(value, 'tp', [(x * side + y, target(x, y)) for x in range(si...  35.7 us
  transfers between devices with their start and end apart: 8, of which 2 were waited for; matrix products, arithmetic and copies ran while one was open for 0% of the time, Pallas kernels for 13%

profile of v1, /device:TPU:97, one launch (start us, length us, event | category | flops | bytes accessed | tf_op | source)
XLA Modules:
  0.0 602.0 jit_solution(186540516265665229)
XLA Ops:
  0.6 379.8 %gather_and_differentiate.1 = (bf16[2560,7168]{1,0:T(8,128)(2,1)}, bf16[2560,7168]{1,0:T(8,128)(2,1)}, bf16[2560,1792]{1,0:T(8,128)(2,1)}, bf16[2560,1792]{1,0:T...) custom-call(bf16[160,7168]{1,0:T(8,128)(2,1)} %x_ref.1, ...), custom_call_target="tpu_custom_call" | custom-call | flops 197300060160 | bytes 370671616 | tf_op jit(solution)/shard_map/gather_and_differentiate/pallas_call | solution.py:430
  380.4 0.1 collective-permute-start.4
  380.6 2.6 collective-permute-start.5
  383.2 0.0 collective-permute-start.6
  383.2 2.7 collective-permute-start.7
  385.9 0.0 collective-permute-start
  385.9 33.8 %collective-permute-done.4.refs_4_ = bf16[3,160,1792]{2,1,0:T(8,128)(2,1)} collective-permute-done((bf16[3,160,1792]{2,1,0:T(8,128)(2,1)}, bf16[3,160,1792]{2,1,0:T(8,128)(2,1)}, u32[]{:S(2)}, u32[]{:S(2)}) %collective-permute-start.4) | collective-permute-done | bytes 1720352 | tf_op jit(solution)/shard_map/ppermute | solution.py:475
  419.7 0.0 collective-permute-start.1
  419.7 0.0 collective-permute-done.5.refs_5_
  419.7 0.2 collective-permute-start.2
  419.9 1.9 collective-permute-done.6.refs_6_
  421.8 0.6 collective-permute-start.3
  422.4 76.6 %shard_map.76 = (bf16[7168,1792]{1,0:T(8,128)(2,1)}, bf16[1792,7168]{1,0:T(8,128)(2,1)}) custom-call(bf16[2560,7168]{1,0:T(8,128)(2,1)} %get-tuple-element.46.x_ref, bf16[2560,1792]{1,0:T(8,128)(2,1)} %get-tuple-element.47.d_pre_ref, bf16[1792,7168]{1,0:T(8,128)(2,1)} %get-tuple-element.48.dw_down_in), custom_call_target="tpu_custom_call" | custom-call | flops 65766686720 | bytes 122945536 | tf_op jit(solution)/shard_map/pallas_call | solution.py:56
  499.0 0.0 collective-permute-done.7.refs_7_
  499.0 0.0 collective-permute-done.refs_0_
  499.0 0.0 collective-permute-done.1.refs_1_
  499.0 0.0 collective-permute-done.2.refs_2_
  499.0 0.0 collective-permute-done.3.refs_3_
  499.0 99.8 %finish_scatter.1 = bf16[160,7168]{1,0:T(8,128)(2,1)} custom-call(bf16[4,160,1792]{2,1,0:T(8,128)(2,1)} %collective-permute-done.refs_0_, bf16[4,160,1792]{2,1,0:T(8,128)(2,1)} %collective-permute-done.1.refs_1_, bf16[4,160,1792]{2,1,0:T(8,128)(2,1)} %collective-permute-done.2.refs_2_, bf16[4,160,1792]{2,1,0:T(8,128)(2,1)} %collective-permute-done.3.refs_3_, ...), custom_call_target="tpu_custom_call" | custom-call | flops 9175040 | bytes 68812800 | tf_op jit(solution)/shard_map/finish_scatter/pallas_call | solution.py:608
  598.8 3.2 copy.9
Async XLA Ops:
  380.4 39.3 %collective-permute-start.4 = (bf16[3,160,1792]{2,1,0:T(8,128)(2,1)}, bf16[3,160,1792]{2,1,0:T(8,128)(2,1)}, u32[]{:S(2)}, u32[]{:S(2)}) collective-permute-start(bf16[3,160,1792]{2,1,0:T(8,128)(2,1)} %get-tuple-element.38), channel_id=1, source_target_pairs={{0,4},{1,5},{2,6},{3,7},{4,8},{5,9},{6,10},{7,11},{8,12},{9,13},{1... | collective-permute-start | bytes 5160968 | tf_op jit(solution)/shard_map/ppermute | solution.py:475
  380.6 39.2 %collective-permute-start.5 = (bf16[3,160,1792]{2,1,0:T(8,128)(2,1)}, bf16[3,160,1792]{2,1,0:T(8,128)(2,1)}, u32[]{:S(2)}, u32[]{:S(2)}) collective-permute-start(bf16[3,160,1792]{2,1,0:T(8,128)(2,1)} %get-tuple-element.39), channel_id=1, source_target_pairs={{0,12},{1,13},{2,14},{3,15},{4,0},{5,1},{6,2},{7,3},{8,4},{9,5},{1... | collective-permute-start | bytes 5160968 | tf_op jit(solution)/shard_map/ppermute | solution.py:475
  383.2 38.6 %collective-permute-start.6 = (bf16[3,160,1792]{2,1,0:T(8,128)(2,1)}, bf16[3,160,1792]{2,1,0:T(8,128)(2,1)}, u32[]{:S(2)}, u32[]{:S(2)}) collective-permute-start(bf16[3,160,1792]{2,1,0:T(8,128)(2,1)} %get-tuple-element.40), channel_id=1, source_target_pairs={{0,1},{1,2},{2,3},{3,0},{4,5},{5,6},{6,7},{7,4},{8,9},{9,10},{10,1... | collective-permute-start | bytes 5160968 | tf_op jit(solution)/shard_map/ppermute | solution.py:475
  383.2 115.8 %collective-permute-start.7 = (bf16[3,160,1792]{2,1,0:T(8,128)(2,1)}, bf16[3,160,1792]{2,1,0:T(8,128)(2,1)}, u32[]{:S(2)}, u32[]{:S(2)}) collective-permute-start(bf16[3,160,1792]{2,1,0:T(8,128)(2,1)} %get-tuple-element.41), channel_id=1, source_target_pairs={{0,3},{1,0},{2,1},{3,2},{4,7},{5,4},{6,5},{7,6},{8,11},{9,8},{10,9... | collective-permute-start | bytes 5160968 | tf_op jit(solution)/shard_map/ppermute | solution.py:475
  385.9 113.1 %collective-permute-start = (bf16[4,160,1792]{2,1,0:T(8,128)(2,1)}, bf16[4,160,1792]{2,1,0:T(8,128)(2,1)}, u32[]{:S(2)}, u32[]{:S(2)}) collective-permute-start(bf16[4,160,1792]{2,1,0:T(8,128)(2,1)} %get-tuple-element.34), channel_id=1, source_target_pairs={{0,4},{1,5},{2,6},{3,7},{4,8},{5,9},{6,10},{7,11},{8,12},{9,13},{1... | collective-permute-start | bytes 6881288 | tf_op jit(solution)/shard_map/ppermute | solution.py:475
  419.7 79.3 %collective-permute-start.1 = (bf16[4,160,1792]{2,1,0:T(8,128)(2,1)}, bf16[4,160,1792]{2,1,0:T(8,128)(2,1)}, u32[]{:S(2)}, u32[]{:S(2)}) collective-permute-start(bf16[4,160,1792]{2,1,0:T(8,128)(2,1)} %get-tuple-element.35), channel_id=1, source_target_pairs={{0,12},{1,13},{2,14},{3,15},{4,0},{5,1},{6,2},{7,3},{8,4},{9,5},{1... | collective-permute-start | bytes 6881288 | tf_op jit(solution)/shard_map/ppermute | solution.py:475
  419.7 79.3 %collective-permute-start.2 = (bf16[4,160,1792]{2,1,0:T(8,128)(2,1)}, bf16[4,160,1792]{2,1,0:T(8,128)(2,1)}, u32[]{:S(2)}, u32[]{:S(2)}) collective-permute-start(bf16[4,160,1792]{2,1,0:T(8,128)(2,1)} %get-tuple-element.36), channel_id=1, source_target_pairs={{0,1},{1,2},{2,3},{3,0},{4,5},{5,6},{6,7},{7,4},{8,9},{9,10},{10,1... | collective-permute-start | bytes 6881288 | tf_op jit(solution)/shard_map/ppermute | solution.py:475
  421.8 77.2 %collective-permute-start.3 = (bf16[4,160,1792]{2,1,0:T(8,128)(2,1)}, bf16[4,160,1792]{2,1,0:T(8,128)(2,1)}, u32[]{:S(2)}, u32[]{:S(2)}) collective-permute-start(bf16[4,160,1792]{2,1,0:T(8,128)(2,1)} %get-tuple-element.37), channel_id=1, source_target_pairs={{0,3},{1,0},{2,1},{3,2},{4,7},{5,4},{6,5},{7,6},{8,11},{9,8},{10,9... | collective-permute-start | bytes 6881288 | tf_op jit(solution)/shard_map/ppermute | solution.py:475

commit v2 on v1

--- a/solution.py
+++ b/solution.py
@@ -475,13 +475,23 @@
     return lax.ppermute(value, "tp", [(x * side + y, target(x, y)) for x in range(side) for y in range(side)])
 
 
+def links_of_quarters():
+    takes = {}
+    for axis, other in (("y", "x"), ("x", "y")):
+        (up, down), (cross_up, cross_down) = UP_DOWN[axis], UP_DOWN[other]
+        high, low = (0, 1) if axis == "y" else (2, 3)
+        takes[high] = up, down, cross_up, cross_down
+        takes[low] = down, up, cross_down, cross_up
+    return takes
+
+
 def scatter_kernel(side, *refs):
-    relay, direct, direct_last, later, own_terms = (refs[4 * i : 4 * i + 4] for i in range(5))
+    relay, direct, later, own_terms = (refs[4 * i : 4 * i + 4] for i in range(4))
     (
-        dx_ref, later_got, last_got, cross_got, later_out, cross_out, exact_in, narrow_in, sums, dx_buf,
-        later_send, later_recv, last_send, last_recv, cross_send, cross_recv, exact_sem, narrow_sem, dx_sem,
-    ) = refs[20:]
-    rows, quarter = dx_buf.shape[1:]
+        kept_ref, last_ref, later_got, cross_got, later_out, cross_out, exact_in, narrow_in, sums,
+        later_send, later_recv, cross_send, cross_recv, exact_sem, narrow_sem, kept_sem,
+    ) = refs[16:]
+    rows, quarter = exact_in.shape[1:]
     t = lax.axis_index("tp")
     me = lax.div(t, side), lax.rem(t, side)
     barrier_with_neighbours(me, side)
@@ -498,27 +508,21 @@
             device_id_type=MESH,
         )
 
-    last_copies = [
-        remote(link, direct_last[link], last_got.at[link], last_send.at[link], last_recv.at[link]) for link in range(4)
-    ]
     later_copies = {
         (link, j): remote(link, later_out.at[link, j], later_got.at[link, j], later_send.at[link, j], later_recv.at[link, j])
         for link in range(4)
         for j in range(side)
     }
-    for c in last_copies:
-        c.start()
-
-    takes = {}
-    for axis, other in (("y", "x"), ("x", "y")):
-        (up, down), (cross_up, cross_down) = UP_DOWN[axis], UP_DOWN[other]
-        high, low = (0, 1) if axis == "y" else (2, 3)
-        takes[high] = up, down, cross_up, cross_down
-        takes[low] = down, up, cross_down, cross_up
+    takes = links_of_quarters()
     step = lambda link: 1 if link in (0, 2) else side - 1
+    columns = [pl.ds(q * quarter, quarter) for q in range(4)]
     cross_copies = {
         (q, k): remote(
-            takes[q][3 if k == 1 else 2], cross_out.at[q, k], cross_got.at[q, k], cross_send.at[q, k], cross_recv.at[q, k]
+            takes[q][3 if k == 1 else 2],
+            cross_out.at[q, k],
+            last_ref.at[:, columns[q]] if k == 2 else cross_got.at[q, k],
+            cross_send.at[q, k],
+            cross_recv.at[q, k],
         )
         for q in range(4)
         for k in range(3)
@@ -566,14 +570,11 @@
             later_copies[which, j].start()
             continue
         q = which
-        main, side_link, _, near_link = takes[q]
+        main, _, _, near_link = takes[q]
         later_copies[main, j].wait_recv()
-        if narrow is None:
-            last_copies[side_link].wait_recv()
-            arrived = last_got.at[side_link]
-        else:
-            arrived = narrow_in.at[slot]
-        parts = exact, later_got.at[main, j], arrived
+        parts = [exact, later_got.at[main, j]]
+        if narrow is not None:
+            parts.append(narrow_in.at[slot])
         if j == 2:
             add(cross_out.at[q, 0], *parts)
             cross_copies[q, 0].start()
@@ -589,17 +590,18 @@
     outs = []
     for q in range(4):
         cross_copies[q, 1].wait_recv()
-        cross_copies[q, 2].wait_recv()
-        add(dx_buf.at[q], sums.at[q, 0], cross_got.at[q, 2], cross_got.at[q, 1])
-        outs.append(pltpu.make_async_copy(dx_buf.at[q], dx_ref.at[:, pl.ds(q * quarter, quarter)], dx_sem.at[q]))
+        add(sums.at[q, 1], sums.at[q, 0], cross_got.at[q, 1])
+        outs.append(pltpu.make_async_copy(sums.at[q, 1], kept_ref.at[:, columns[q]], kept_sem.at[q]))
         outs[-1].start()
     for c in outs:
         c.wait()
-    for c in [*last_copies, *later_copies.values(), *cross_copies.values()]:
+    for q in range(4):
+        cross_copies[q, 2].wait_recv()
+    for c in [*later_copies.values(), *cross_copies.values()]:
         c.wait_send()
 
 
-def finish_scatter(relay, direct, direct_last, later, own_terms):
+def sum_and_scatter(relay, direct, later, own_terms):
     side, rows, quarter = relay[0].shape
     kind = relay[0].dtype
     any_space = pl.BlockSpec(memory_space=pl.ANY)
@@ -607,23 +609,19 @@
     piece, slots = (rows, quarter), 4
     return pl.pallas_call(
         functools.partial(scatter_kernel, side),
-        out_shape=jax.ShapeDtypeStruct((rows, 4 * quarter), kind),
-        in_specs=[any_space] * 20,
-        out_specs=any_space,
+        out_shape=[jax.ShapeDtypeStruct((rows, 4 * quarter), t) for t in (jnp.float32, kind)],
+        in_specs=[any_space] * 16,
+        out_specs=[any_space] * 2,
         scratch_shapes=[
             pltpu.VMEM((4, side, *piece), kind),
-            pltpu.VMEM((4, *piece), kind),
-            pltpu.VMEM((4, 3, *piece), kind),
+            pltpu.VMEM((4, 2, *piece), kind),
             pltpu.VMEM((4, side, *piece), kind),
             pltpu.VMEM((4, 3, *piece), kind),
             pltpu.VMEM((slots, *piece), jnp.float32),
             pltpu.VMEM((slots, *piece), kind),
             pltpu.VMEM((4, 2, *piece), jnp.float32),
-            pltpu.VMEM((4, *piece), kind),
             dma((4, side)),
             dma((4, side)),
-            dma((4,)),
-            dma((4,)),
             dma((4, 3)),
             dma((4, 3)),
             dma((slots,)),
@@ -636,8 +634,34 @@
         cost_estimate=pl.CostEstimate(
             flops=8 * side * rows * quarter, bytes_accessed=60 * side * rows * quarter, transcendentals=0
         ),
-        name="finish_scatter",
-    )(*relay, *direct, *direct_last, *later, *own_terms)
+        name="sum_and_scatter",
+    )(*relay, *direct, *later, *own_terms)
+
+
+def finish_kernel(kept_ref, last_ref, *refs):
+    dx_ref = refs[-1]
+    for q, direct in enumerate(refs[:-1]):
+
+        @pl.when(pl.program_id(0) == q)
+        def _():
+            total = kept_ref[...] + direct[...].astype(jnp.float32) + last_ref[...].astype(jnp.float32)
+            dx_ref[...] = total.astype(dx_ref.dtype)
+
+
+def finish_dx(kept, last, direct_last):
+    rows, depth = kept.shape
+    piece = (rows, depth // 4)
+    column = pl.BlockSpec(piece, lambda q: (0, q))
+    takes = links_of_quarters()
+    return pl.pallas_call(
+        finish_kernel,
+        grid=(4,),
+        in_specs=[column, column] + [pl.BlockSpec(piece, lambda q: (0, 0))] * 4,
+        out_specs=column,
+        out_shape=jax.ShapeDtypeStruct(kept.shape, last.dtype),
+        cost_estimate=pl.CostEstimate(flops=2 * rows * depth, bytes_accessed=10 * rows * depth, transcendentals=0),
+        name="finish_dx",
+    )(kept, last, *(direct_last[takes[q][1]] for q in range(4)))
 
 
 def solution(mesh):
@@ -650,9 +674,10 @@
         )
         relay = [shift(block, link, side) for link, block in enumerate(relay)]
         direct = [shift(block, link, side) for link, block in enumerate(direct)]
+        direct_last = [shift(block, link, side) for link, block in enumerate(direct_last)]
         dw_in, dw_down = dw_in_and_copy(x_all, d_pre, dw_down, 2 * TILE)
         dw_in, dw_down, later = lax.optimization_barrier((dw_in, dw_down, later))
-        dx = finish_scatter(relay, direct, direct_last, later, own_terms)
+        dx = finish_dx(*sum_and_scatter(relay, direct, later, own_terms), direct_last)
         return dx, dw_in, dw_down
 
     tokens = P(("dp", "tp"), None)

time: 606 us -> 652 us (1.076)
  waiting for transfers between devices: 35.7 us -> 84.6 us
    ppermute x8 -> x12, waiting for transfers between devices: 35.7 us -> 84.6 us  [shift(): lax.ppermute(value, 'tp', [(x * side + y, target(x, y)) for x in range(si...]
    pallas_call x1 -> x2, Pallas kernels: 99.8 us -> 94.1 us  [the longest x1 88.4 us: sum_and_scatter(): pl.pallas_call(functools.partial(scatter_kernel, side), out_shape=[jax.Sh...]
  transfers between devices with their start and end apart: 8 -> 12, of which waited for: 2 -> 2; matrix products, arithmetic and copies ran while one was open for 0% -> 0% of each run, Pallas kernels for 13% -> 25%
where the time goes in v2:
time: 652 us; the launch traced here: 648 us
  Pallas kernels  550 us (84%)
  waiting for transfers between devices  84.6 us (13%)
  starting transfers between devices  12.3 us (2%)
    pallas_call x1, Pallas kernels, gather_and_differentiate(): pl.pallas_call(functools.partial(gather_kernel, side), out_shape=[like((g...  380 us
    pallas_call x1, Pallas kernels, sum_and_scatter(): pl.pallas_call(functools.partial(scatter_kernel, side), out_shape=[jax.Sh...  88.4 us
    ppermute x12, waiting for transfers between devices, shift(): lax.ppermute(value, 'tp', [(x * side + y, target(x, y)) for x in range(si...  84.6 us
    pallas_call x1, Pallas kernels, dw_in_and_copy(): pl.pallas_call(dw_in_kernel, grid=(steps,), in_specs=[pl.BlockSpec((token...  76.6 us
  transfers between devices with their start and end apart: 12, of which 2 were waited for; matrix products, arithmetic and copies ran while one was open for 0% of the time, Pallas kernels for 25%

profile of v2, /device:TPU:97, one launch (start us, length us, event | category | flops | bytes accessed | tf_op | source)
XLA Modules:
  0.0 648.0 jit_solution(12492005888078564370)
XLA Ops:
  0.6 379.8 %gather_and_differentiate.1 = (bf16[2560,7168]{1,0:T(8,128)(2,1)}, bf16[2560,7168]{1,0:T(8,128)(2,1)}, bf16[2560,1792]{1,0:T(8,128)(2,1)}, bf16[2560,1792]{1,0:T...) custom-call(bf16[160,7168]{1,0:T(8,128)(2,1)} %x_ref.1, ...), custom_call_target="tpu_custom_call" | custom-call | flops 197300060160 | bytes 370671616 | tf_op jit(solution)/shard_map/gather_and_differentiate/pallas_call | solution.py:430
  380.4 0.1 collective-permute-start.4
  380.6 2.6 collective-permute-start.5
  383.2 0.0 collective-permute-start
  383.2 2.7 collective-permute-start.1
  385.9 0.0 collective-permute-start.2
  385.9 33.8 %collective-permute-done.4.refs_4_ = bf16[3,160,1792]{2,1,0:T(8,128)(2,1)} collective-permute-done((bf16[3,160,1792]{2,1,0:T(8,128)(2,1)}, bf16[3,160,1792]{2,1,0:T(8,128)(2,1)}, u32[]{:S(2)}, u32[]{:S(2)}) %collective-permute-start.4) | collective-permute-done | bytes 1720352 | tf_op jit(solution)/shard_map/ppermute | solution.py:475
  419.7 0.0 collective-permute-start.6
  419.7 0.0 collective-permute-done.5.refs_5_
  419.7 2.7 collective-permute-start.7
  422.4 50.7 %collective-permute-done.6.refs_6_ = bf16[3,160,1792]{2,1,0:T(8,128)(2,1)} collective-permute-done((bf16[3,160,1792]{2,1,0:T(8,128)(2,1)}, bf16[3,160,1792]{2,1,0:T(8,128)(2,1)}, u32[]{:S(2)}, u32[]{:S(2)}) %collective-permute-start.6) | collective-permute-done | bytes 1720352 | tf_op jit(solution)/shard_map/ppermute | solution.py:475
  473.1 0.0 collective-permute-start.8
  473.1 0.0 collective-permute-done.7.refs_7_
  473.1 1.5 collective-permute-start.9
  474.6 0.3 collective-permute-start.10
  474.9 1.2 collective-permute-start.11
  476.0 0.0 collective-permute-done.2.refs_2_
  476.0 1.2 collective-permute-start.3
  477.3 76.6 %shard_map.76 = (bf16[7168,1792]{1,0:T(8,128)(2,1)}, bf16[1792,7168]{1,0:T(8,128)(2,1)}) custom-call(bf16[2560,7168]{1,0:T(8,128)(2,1)} %get-tuple-element.44.x_ref, bf16[2560,1792]{1,0:T(8,128)(2,1)} %get-tuple-element.45.d_pre_ref, bf16[1792,7168]{1,0:T(8,128)(2,1)} %get-tuple-element.46.dw_down_in), custom_call_target="tpu_custom_call" | custom-call | flops 65766686720 | bytes 122945536 | tf_op jit(solution)/shard_map/pallas_call | solution.py:56
  553.8 0.0 collective-permute-done.3.refs_3_
  553.8 88.4 %sum_and_scatter.1 = (f32[160,7168]{1,0:T(8,128)}, bf16[160,7168]{1,0:T(8,128)(2,1)}) custom-call(bf16[4,160,1792]{2,1,0:T(8,128)(2,1)} %collective-permute-done.refs_0_, bf16[4,160,1792]{2,1,0:T(8,128)(2,1)} %collective-permute-done.1.refs_1_, bf16[4,160,1792]{2,1,0:T(8,128)(2,1)} %collective-permute-done.2.refs_2_, ...), custom_call_target="tpu_custom_call" | custom-call | flops 9175040 | bytes 68812800 | tf_op jit(solution)/shard_map/sum_and_scatter/pallas_call | solution.py:610
  642.2 0.0 collective-permute-done.9.refs_1_
  642.3 0.0 collective-permute-done.10.refs_2_
  642.3 5.7 finish_dx.1
  (4 shorter events, 0.0 us)
Async XLA Ops:
  380.4 39.3 %collective-permute-start.4 = (bf16[3,160,1792]{2,1,0:T(8,128)(2,1)}, bf16[3,160,1792]{2,1,0:T(8,128)(2,1)}, u32[]{:S(2)}, u32[]{:S(2)}) collective-permute-start(bf16[3,160,1792]{2,1,0:T(8,128)(2,1)} %get-tuple-element.40), channel_id=1, source_target_pairs={{0,4},{1,5},{2,6},{3,7},{4,8},{5,9},{6,10},{7,11},{8,12},{9,13},{1... | collective-permute-start | bytes 5160968 | tf_op jit(solution)/shard_map/ppermute | solution.py:475
  380.6 39.2 %collective-permute-start.5 = (bf16[3,160,1792]{2,1,0:T(8,128)(2,1)}, bf16[3,160,1792]{2,1,0:T(8,128)(2,1)}, u32[]{:S(2)}, u32[]{:S(2)}) collective-permute-start(bf16[3,160,1792]{2,1,0:T(8,128)(2,1)} %get-tuple-element.41), channel_id=1, source_target_pairs={{0,12},{1,13},{2,14},{3,15},{4,0},{5,1},{6,2},{7,3},{8,4},{9,5},{1... | collective-permute-start | bytes 5160968 | tf_op jit(solution)/shard_map/ppermute | solution.py:475
  383.2 91.4 %collective-permute-start = (bf16[4,160,1792]{2,1,0:T(8,128)(2,1)}, bf16[4,160,1792]{2,1,0:T(8,128)(2,1)}, u32[]{:S(2)}, u32[]{:S(2)}) collective-permute-start(bf16[4,160,1792]{2,1,0:T(8,128)(2,1)} %get-tuple-element.36), channel_id=1, source_target_pairs={{0,4},{1,5},{2,6},{3,7},{4,8},{5,9},{6,10},{7,11},{8,12},{9,13},{1... | collective-permute-start | bytes 6881288 | tf_op jit(solution)/shard_map/ppermute | solution.py:475
  383.2 91.6 %collective-permute-start.1 = (bf16[4,160,1792]{2,1,0:T(8,128)(2,1)}, bf16[4,160,1792]{2,1,0:T(8,128)(2,1)}, u32[]{:S(2)}, u32[]{:S(2)}) collective-permute-start(bf16[4,160,1792]{2,1,0:T(8,128)(2,1)} %get-tuple-element.37), channel_id=1, source_target_pairs={{0,12},{1,13},{2,14},{3,15},{4,0},{5,1},{6,2},{7,3},{8,4},{9,5},{1... | collective-permute-start | bytes 6881288 | tf_op jit(solution)/shard_map/ppermute | solution.py:475
  385.9 90.2 %collective-permute-start.2 = (bf16[4,160,1792]{2,1,0:T(8,128)(2,1)}, bf16[4,160,1792]{2,1,0:T(8,128)(2,1)}, u32[]{:S(2)}, u32[]{:S(2)}) collective-permute-start(bf16[4,160,1792]{2,1,0:T(8,128)(2,1)} %get-tuple-element.38), channel_id=1, source_target_pairs={{0,1},{1,2},{2,3},{3,0},{4,5},{5,6},{6,7},{7,4},{8,9},{9,10},{10,1... | collective-permute-start | bytes 6881288 | tf_op jit(solution)/shard_map/ppermute | solution.py:475
  419.7 53.4 %collective-permute-start.6 = (bf16[3,160,1792]{2,1,0:T(8,128)(2,1)}, bf16[3,160,1792]{2,1,0:T(8,128)(2,1)}, u32[]{:S(2)}, u32[]{:S(2)}) collective-permute-start(bf16[3,160,1792]{2,1,0:T(8,128)(2,1)} %get-tuple-element.42), channel_id=1, source_target_pairs={{0,1},{1,2},{2,3},{3,0},{4,5},{5,6},{6,7},{7,4},{8,9},{9,10},{10,1... | collective-permute-start | bytes 5160968 | tf_op jit(solution)/shard_map/ppermute | solution.py:475
  419.7 53.4 %collective-permute-start.7 = (bf16[3,160,1792]{2,1,0:T(8,128)(2,1)}, bf16[3,160,1792]{2,1,0:T(8,128)(2,1)}, u32[]{:S(2)}, u32[]{:S(2)}) collective-permute-start(bf16[3,160,1792]{2,1,0:T(8,128)(2,1)} %get-tuple-element.43), channel_id=1, source_target_pairs={{0,3},{1,0},{2,1},{3,2},{4,7},{5,4},{6,5},{7,6},{8,11},{9,8},{10,9... | collective-permute-start | bytes 5160968 | tf_op jit(solution)/shard_map/ppermute | solution.py:475
  473.1 169.1 %collective-permute-start.8 = (bf16[160,1792]{1,0:T(8,128)(2,1)}, bf16[160,1792]{1,0:T(8,128)(2,1)}, u32[]{:S(2)}, u32[]{:S(2)}) collective-permute-start(bf16[160,1792]{1,0:T(8,128)(2,1)} %get-tuple-element.63), channel_id=1, source_target_pairs={{0,3},{1,0},{2,1},{3,2},{4,7},{5,4},{6,5},{7,6},{8,11},{9,8},{10,9... | collective-permute-start | bytes 1720328 | tf_op jit(solution)/shard_map/ppermute | solution.py:475
  473.1 169.2 %collective-permute-start.9 = (bf16[160,1792]{1,0:T(8,128)(2,1)}, bf16[160,1792]{1,0:T(8,128)(2,1)}, u32[]{:S(2)}, u32[]{:S(2)}) collective-permute-start(bf16[160,1792]{1,0:T(8,128)(2,1)} %get-tuple-element.64), channel_id=1, source_target_pairs={{0,1},{1,2},{2,3},{3,0},{4,5},{5,6},{6,7},{7,4},{8,9},{9,10},{10,1... | collective-permute-start | bytes 1720328 | tf_op jit(solution)/shard_map/ppermute | solution.py:475
  474.6 167.7 %collective-permute-start.10 = (bf16[160,1792]{1,0:T(8,128)(2,1)}, bf16[160,1792]{1,0:T(8,128)(2,1)}, u32[]{:S(2)}, u32[]{:S(2)}) collective-permute-start(bf16[160,1792]{1,0:T(8,128)(2,1)} %get-tuple-element.65), channel_id=1, source_target_pairs={{0,12},{1,13},{2,14},{3,15},{4,0},{5,1},{6,2},{7,3},{8,4},{9,5},{1... | collective-permute-start | bytes 1720328 | tf_op jit(solution)/shard_map/ppermute | solution.py:475
  474.9 167.4 %collective-permute-start.11 = (bf16[160,1792]{1,0:T(8,128)(2,1)}, bf16[160,1792]{1,0:T(8,128)(2,1)}, u32[]{:S(2)}, u32[]{:S(2)}) collective-permute-start(bf16[160,1792]{1,0:T(8,128)(2,1)} %get-tuple-element.66), channel_id=1, source_target_pairs={{0,4},{1,5},{2,6},{3,7},{4,8},{5,9},{6,10},{7,11},{8,12},{9,13},{1... | collective-permute-start | bytes 1720328 | tf_op jit(solution)/shard_map/ppermute | solution.py:475
  476.0 77.8 %collective-permute-start.3 = (bf16[4,160,1792]{2,1,0:T(8,128)(2,1)}, bf16[4,160,1792]{2,1,0:T(8,128)(2,1)}, u32[]{:S(2)}, u32[]{:S(2)}) collective-permute-start(bf16[4,160,1792]{2,1,0:T(8,128)(2,1)} %get-tuple-element.39), channel_id=1, source_target_pairs={{0,3},{1,0},{2,1},{3,2},{4,7},{5,4},{6,5},{7,6},{8,11},{9,8},{10,9... | collective-permute-start | bytes 6881288 | tf_op jit(solution)/shard_map/ppermute | solution.py:475

commit v3 on v2

--- a/solution.py
+++ b/solution.py
@@ -80,6 +80,24 @@
 STEPS = ((1, 0), (-1, 0), (0, 1), (0, -1))
 
 
+class Torus:
+    def __init__(self, side):
+        self.side = side
+        t, self.odd = lax.axis_index("tp"), lax.rem(lax.axis_index("dp"), 2)
+        x, y = lax.div(t, side), lax.rem(t, side)
+        self.me = tuple(m + self.odd * (self.mirror(n) - m) for m, n in ((x, y), (y, x)))
+
+    def mirror(self, n):
+        return lax.rem(self.side - n, self.side)
+
+    def index(self, x, y):
+        straight, mirrored = x * self.side + y, self.mirror(y) * self.side + self.mirror(x)
+        return straight + self.odd * (mirrored - straight)
+
+    def at(self, ox, oy):
+        return self.index(*(lax.rem(m + o + self.side, self.side) for m, o in zip(self.me, (ox, oy))))
+
+
 def pieces_of(link):
     along_x, up = link < 2, link % 2 == 0
     mine = (0, 1) if along_x else (2, 3)
@@ -101,9 +119,9 @@
 
 
 class Gather:
-    def __init__(self, own, every, send_sem, recv_sem, me, side):
+    def __init__(self, own, every, send_sem, recv_sem, torus):
         self.own, self.every, self.send_sem, self.recv_sem = own, every, send_sem, recv_sem
-        self.me, self.side, self.rows = me, side, own.shape[0]
+        self.torus, self.rows = torus, own.shape[0]
         self.unit = self.rows // 4
         self.sent, self.pending = [], {}
         for link, (dx, dy) in enumerate(STEPS):
@@ -115,24 +133,19 @@
         self.arrival = dict(self.pending)
 
     def key(self, ox, oy, q):
-        return ox % self.side, oy % self.side, q
-
-    def start_row(self, ox, oy):
-        x, y = (lax.rem(m + (o % self.side), self.side) for m, o in zip(self.me, (ox, oy)))
-        return pl.multiple_of((x * self.side + y) * self.rows, self.unit)
+        return ox % self.torus.side, oy % self.torus.side, q
 
     def place(self, ox, oy, q):
-        return self.every.at[pl.ds(pl.multiple_of(self.start_row(ox, oy) + q * self.unit, 8), self.unit)]
+        start = self.torus.at(*self.key(ox, oy, q)[:2]) * self.rows + q * self.unit
+        return self.every.at[pl.ds(pl.multiple_of(start, 8), self.unit)]
 
     def copy(self, link, k, source, target):
-        dx, dy = STEPS[link]
-        x, y = (lax.rem(m + d + self.side, self.side) for m, d in zip(self.me, (dx, dy)))
         return pltpu.make_async_remote_copy(
             src_ref=source,
             dst_ref=target,
             send_sem=self.send_sem.at[link, k],
             recv_sem=self.recv_sem.at[link, k],
-            device_id={"tp": x * self.side + y},
+            device_id={"tp": self.torus.at(*STEPS[link])},
             device_id_type=MESH,
         )
 
@@ -172,11 +185,15 @@
         for q in range(4):
             self.wait(ox, oy, q)
 
+    def finish_sends(self):
+        for link, k, place in self.sent:
+            self.copy(link, k, place, place).wait_send()
+        self.sent.clear()
+
     def finish(self):
         for key in list(self.pending):
             self.wait(*key)
-        for link, k, place in self.sent:
-            self.copy(link, k, place, place).wait_send()
+        self.finish_sends()
 
 
 UP_DOWN = {"y": (2, 3), "x": (0, 1)}
@@ -191,11 +208,10 @@
     }
 
 
-def barrier_with_neighbours(me, side):
+def barrier_with_neighbours(torus):
     barrier = pltpu.get_barrier_semaphore()
-    for dx, dy in STEPS:
-        x, y = (lax.rem(m + d + side, side) for m, d in zip(me, (dx, dy)))
-        pl.semaphore_signal(barrier, inc=1, device_id={"tp": x * side + y}, device_id_type=MESH)
+    for offset in STEPS:
+        pl.semaphore_signal(barrier, inc=1, device_id={"tp": torus.at(*offset)}, device_id_type=MESH)
     pl.semaphore_wait(barrier, len(STEPS))
 
 
@@ -215,12 +231,11 @@
     rows, depth = dy_ref.shape
     width = pre_ref.shape[1]
     quarter = depth // 4
-    t = lax.axis_index("tp")
-    me = lax.div(t, side), lax.rem(t, side)
-    barrier_with_neighbours(me, side)
-
-    dys = Gather(dy_ref, dy_all, dy_send, dy_recv, me, side)
-    xs = Gather(x_ref, x_all, x_send, x_recv, me, side)
+    torus = Torus(side)
+    barrier_with_neighbours(torus)
+
+    dys = Gather(dy_ref, dy_all, dy_send, dy_recv, torus)
+    xs = Gather(x_ref, x_all, x_send, x_recv, torus)
     dys.send(0)
 
     def load_quarter(q):
@@ -238,8 +253,7 @@
             weights[k, :, tile_at(n)] = dy_buf[0:TILE, k * quarter : (k + 1) * quarter].T
 
     def rows_of(ox, oy):
-        x, y = lax.rem(me[0] + ox + side, side), lax.rem(me[1] + oy + side, side)
-        return pl.ds(pl.multiple_of((x * side + y) * rows, rows), rows)
+        return pl.ds(pl.multiple_of(torus.at(ox, oy) * rows, rows), rows)
 
     def wrap(offset):
         return offset % side if isinstance(offset, int) else lax.rem(offset + side, side)
@@ -412,6 +426,7 @@
     for n in (count - 2, count - 1):
         store_tile(n, n % 2).wait()
     dys.finish()
+    xs.finish_sends()
     xs.finish()
 
 
@@ -469,10 +484,19 @@
     return *outs[:5], *(outs[5 + 4 * i : 9 + 4 * i] for i in range(5))
 
 
-def shift(value, link, side):
+def shift(value, link, mesh):
+    group = mesh.shape["tp"]
+    side = math.isqrt(group)
     dx, dy = STEPS[link]
-    target = lambda x, y: (x + dx) % side * side + (y + dy) % side
-    return lax.ppermute(value, "tp", [(x * side + y, target(x, y)) for x in range(side) for y in range(side)])
+    pairs = []
+    for g in range(mesh.shape["dp"]):
+        index = (lambda x, y: -y % side * side + -x % side) if g % 2 else (lambda x, y: x * side + y)
+        pairs += [
+            (g * group + index(x, y), g * group + index((x + dx) % side, (y + dy) % side))
+            for x in range(side)
+            for y in range(side)
+        ]
+    return lax.ppermute(value, ("dp", "tp"), pairs)
 
 
 def links_of_quarters():
@@ -492,19 +516,16 @@
         later_send, later_recv, cross_send, cross_recv, exact_sem, narrow_sem, kept_sem,
     ) = refs[16:]
     rows, quarter = exact_in.shape[1:]
-    t = lax.axis_index("tp")
-    me = lax.div(t, side), lax.rem(t, side)
-    barrier_with_neighbours(me, side)
+    torus = Torus(side)
+    barrier_with_neighbours(torus)
 
     def remote(link, source, target, send_sem, recv_sem):
-        dx, dy = STEPS[link]
-        x, y = (lax.rem(m + d + side, side) for m, d in zip(me, (dx, dy)))
         return pltpu.make_async_remote_copy(
             src_ref=source,
             dst_ref=target,
             send_sem=send_sem,
             recv_sem=recv_sem,
-            device_id={"tp": x * side + y},
+            device_id={"tp": torus.at(*STEPS[link])},
             device_id_type=MESH,
         )
 
@@ -595,10 +616,10 @@
         outs[-1].start()
     for c in outs:
         c.wait()
+    for c in [*later_copies.values(), *cross_copies.values()]:
+        c.wait_send()
     for q in range(4):
         cross_copies[q, 2].wait_recv()
-    for c in [*later_copies.values(), *cross_copies.values()]:
-        c.wait_send()
 
 
 def sum_and_scatter(relay, direct, later, own_terms):
@@ -639,26 +660,46 @@
 
 
 def finish_kernel(kept_ref, last_ref, *refs):
-    dx_ref = refs[-1]
-    for q, direct in enumerate(refs[:-1]):
-
-        @pl.when(pl.program_id(0) == q)
-        def _():
-            total = kept_ref[...] + direct[...].astype(jnp.float32) + last_ref[...].astype(jnp.float32)
-            dx_ref[...] = total.astype(dx_ref.dtype)
+    direct, (dx_ref, kept, last, owner, dx, kept_sem, last_sem, owner_sem, dx_sem) = refs[:4], refs[4:]
+    quarter = kept.shape[2]
+    columns = [pl.ds(q * quarter, quarter) for q in range(4)]
+    loads = [
+        [
+            pltpu.make_async_copy(kept_ref.at[:, columns[q]], kept.at[q], kept_sem.at[q]),
+            pltpu.make_async_copy(last_ref.at[:, columns[q]], last.at[q], last_sem.at[q]),
+            pltpu.make_async_copy(direct[q], owner.at[q], owner_sem.at[q]),
+        ]
+        for q in range(4)
+    ]
+    for copies in loads:
+        for c in copies:
+            c.start()
+    stores = []
+    for q, copies in enumerate(loads):
+        for c in copies:
+            c.wait()
+        total = kept[q] + owner[q].astype(jnp.float32) + last[q].astype(jnp.float32)
+        dx[q] = total.astype(dx.dtype)
+        stores.append(pltpu.make_async_copy(dx.at[q], dx_ref.at[:, columns[q]], dx_sem.at[q]))
+        stores[-1].start()
+    for c in stores:
+        c.wait()
 
 
 def finish_dx(kept, last, direct_last):
     rows, depth = kept.shape
-    piece = (rows, depth // 4)
-    column = pl.BlockSpec(piece, lambda q: (0, q))
+    pieces = (4, rows, depth // 4)
     takes = links_of_quarters()
+    any_space = pl.BlockSpec(memory_space=pl.ANY)
     return pl.pallas_call(
         finish_kernel,
-        grid=(4,),
-        in_specs=[column, column] + [pl.BlockSpec(piece, lambda q: (0, 0))] * 4,
-        out_specs=column,
+        in_specs=[any_space] * 6,
+        out_specs=any_space,
         out_shape=jax.ShapeDtypeStruct(kept.shape, last.dtype),
+        scratch_shapes=[pltpu.VMEM(pieces, jnp.float32)]
+        + [pltpu.VMEM(pieces, last.dtype)] * 3
+        + [pltpu.SemaphoreType.DMA((4,))] * 4,
+        compiler_params=pltpu.CompilerParams(vmem_limit_bytes=60 * 1024 * 1024),
         cost_estimate=pl.CostEstimate(flops=2 * rows * depth, bytes_accessed=10 * rows * depth, transcendentals=0),
         name="finish_dx",
     )(kept, last, *(direct_last[takes[q][1]] for q in range(4)))
@@ -666,15 +707,14 @@
 
 def solution(mesh):
     group = mesh.shape["tp"]
-    side = math.isqrt(group)
 
     def step(x, dy, pre, w_in, w_down):
         x_all, _, _, d_pre, dw_down, relay, direct, direct_last, later, own_terms = gather_and_differentiate(
             x, dy, pre, w_down, w_in, group
         )
-        relay = [shift(block, link, side) for link, block in enumerate(relay)]
-        direct = [shift(block, link, side) for link, block in enumerate(direct)]
-        direct_last = [shift(block, link, side) for link, block in enumerate(direct_last)]
+        relay = [shift(block, link, mesh) for link, block in enumerate(relay)]
+        direct = [shift(block, link, mesh) for link, block in enumerate(direct)]
+        direct_last = [shift(block, link, mesh) for link, block in enumerate(direct_last)]
         dw_in, dw_down = dw_in_and_copy(x_all, d_pre, dw_down, 2 * TILE)
         dw_in, dw_down, later = lax.optimization_barrier((dw_in, dw_down, later))
         dx = finish_dx(*sum_and_scatter(relay, direct, later, own_terms), direct_last)

time: 652 us -> 653 us (level)
  transfers between devices with their start and end apart: 12 -> 12, of which waited for: 2 -> 3; matrix products, arithmetic and copies ran while one was open for 0% -> 0% of each run, Pallas kernels for 25% -> 26%
where the time goes in v3:
time: 653 us
  Pallas kernels  555 us (85%)
  waiting for transfers between devices  82.2 us (13%)
  starting transfers between devices  15.3 us (2%)
    pallas_call x1, Pallas kernels, gather_and_differentiate(): pl.pallas_call(functools.partial(gather_kernel, side), out_shape=[like((g...  380 us
    pallas_call x1, Pallas kernels, sum_and_scatter(): pl.pallas_call(functools.partial(scatter_kernel, side), out_shape=[jax.Sh...  92.8 us
    ppermute x12, waiting for transfers between devices, shift(): return lax.ppermute(value, ('dp', 'tp'), pairs)  82.2 us
    pallas_call x1, Pallas kernels, dw_in_and_copy(): pl.pallas_call(dw_in_kernel, grid=(steps,), in_specs=[pl.BlockSpec((token...  76.8 us
    ppermute x12, starting transfers between devices, shift(): return lax.ppermute(value, ('dp', 'tp'), pairs)  15.3 us
  transfers between devices with their start and end apart: 12, of which 3 were waited for; matrix products, arithmetic and copies ran while one was open for 0% of the time, Pallas kernels for 26%

profile of v3, /device:TPU:97, one launch (start us, length us, event | category | flops | bytes accessed | tf_op | source)
XLA Modules:
  0.0 653.0 jit_solution(4473867794083423298)
XLA Ops:
  0.6 379.8 %gather_and_differentiate.1 = (bf16[2560,7168]{1,0:T(8,128)(2,1)}, bf16[2560,7168]{1,0:T(8,128)(2,1)}, bf16[2560,1792]{1,0:T(8,128)(2,1)}, bf16[2560,1792]{1,0:T...) custom-call(bf16[160,7168]{1,0:T(8,128)(2,1)} %x_ref.1, ...), custom_call_target="tpu_custom_call" | custom-call | flops 197300060160 | bytes 370671616 | tf_op jit(solution)/shard_map/gather_and_differentiate/pallas_call | solution.py:445
  380.5 0.5 collective-permute-start.4
  380.9 1.1 collective-permute-start.5
  382.0 1.6 collective-permute-start
  383.6 0.0 collective-permute-start.1
  383.6 2.3 collective-permute-start.2
  385.9 16.1 %collective-permute-done.4.refs_4_ = bf16[3,160,1792]{2,1,0:T(8,128)(2,1)} collective-permute-done((bf16[3,160,1792]{2,1,0:T(8,128)(2,1)}, bf16[3,160,1792]{2,1,0:T(8,128)(2,1)}, u32[]{:S(2)}, u32[]{:S(2)}) %collective-permute-start.4) | collective-permute-done | bytes 1720352 | tf_op jit(solution)/shard_map/ppermute | solution.py:499
  402.0 0.5 collective-permute-start.6
  402.5 11.7 %collective-permute-done.5.refs_5_ = bf16[3,160,1792]{2,1,0:T(8,128)(2,1)} collective-permute-done((bf16[3,160,1792]{2,1,0:T(8,128)(2,1)}, bf16[3,160,1792]{2,1,0:T(8,128)(2,1)}, u32[]{:S(2)}, u32[]{:S(2)}) %collective-permute-start.5) | collective-permute-done | bytes 1720352 | tf_op jit(solution)/shard_map/ppermute | solution.py:499
  414.1 3.6 collective-permute-start.7
  417.7 54.5 %collective-permute-done.6.refs_6_ = bf16[3,160,1792]{2,1,0:T(8,128)(2,1)} collective-permute-done((bf16[3,160,1792]{2,1,0:T(8,128)(2,1)}, bf16[3,160,1792]{2,1,0:T(8,128)(2,1)}, u32[]{:S(2)}, u32[]{:S(2)}) %collective-permute-start.6) | collective-permute-done | bytes 1720352 | tf_op jit(solution)/shard_map/ppermute | solution.py:499
  472.2 0.1 collective-permute-start.8
  472.3 0.0 collective-permute-done.7.refs_7_
  472.3 3.0 collective-permute-start.9
  475.3 0.0 collective-permute-done.refs_0_
  475.3 0.0 collective-permute-start.10
  475.3 0.0 collective-permute-done.1.refs_1_
  475.3 2.7 collective-permute-start.11
  478.0 0.0 collective-permute-done.2.refs_2_
  478.0 76.8 %shard_map.76 = (bf16[7168,1792]{1,0:T(8,128)(2,1)}, bf16[1792,7168]{1,0:T(8,128)(2,1)}) custom-call(bf16[2560,7168]{1,0:T(8,128)(2,1)} %get-tuple-element.44.x_ref, bf16[2560,1792]{1,0:T(8,128)(2,1)} %get-tuple-element.45.d_pre_ref, bf16[1792,7168]{1,0:T(8,128)(2,1)} %get-tuple-element.46.dw_down_in), custom_call_target="tpu_custom_call" | custom-call | flops 65766686720 | bytes 122945536 | tf_op jit(solution)/shard_map/pallas_call | solution.py:56
  554.8 0.0 collective-permute-done.3.refs_3_
  554.8 92.8 %sum_and_scatter.1 = (f32[160,7168]{1,0:T(8,128)}, bf16[160,7168]{1,0:T(8,128)(2,1)}) custom-call(bf16[4,160,1792]{2,1,0:T(8,128)(2,1)} %collective-permute-done.refs_0_, bf16[4,160,1792]{2,1,0:T(8,128)(2,1)} %collective-permute-done.1.refs_1_, bf16[4,160,1792]{2,1,0:T(8,128)(2,1)} %collective-permute-done.2.refs_2_, ...), custom_call_target="tpu_custom_call" | custom-call | flops 9175040 | bytes 68812800 | tf_op jit(solution)/shard_map/sum_and_scatter/pallas_call | solution.py:631
  647.7 0.0 collective-permute-done.10.refs_2_
  647.7 5.1 finish_dx.1
  (4 shorter events, 0.0 us)
Async XLA Ops:
  380.5 21.5 %collective-permute-start.4 = (bf16[3,160,1792]{2,1,0:T(8,128)(2,1)}, bf16[3,160,1792]{2,1,0:T(8,128)(2,1)}, u32[]{:S(2)}, u32[]{:S(2)}) collective-permute-start(bf16[3,160,1792]{2,1,0:T(8,128)(2,1)} %get-tuple-element.40), channel_id=1, source_target_pairs={{0,4},{1,5},{2,6},{3,7},{4,8},{5,9},{6,10},{7,11},{8,12},{9,13},{1... | collective-permute-start | bytes 5160968 | tf_op jit(solution)/shard_map/ppermute | solution.py:499
  380.9 33.2 %collective-permute-start.5 = (bf16[3,160,1792]{2,1,0:T(8,128)(2,1)}, bf16[3,160,1792]{2,1,0:T(8,128)(2,1)}, u32[]{:S(2)}, u32[]{:S(2)}) collective-permute-start(bf16[3,160,1792]{2,1,0:T(8,128)(2,1)} %get-tuple-element.41), channel_id=1, source_target_pairs={{0,12},{1,13},{2,14},{3,15},{4,0},{5,1},{6,2},{7,3},{8,4},{9,5},{1... | collective-permute-start | bytes 5160968 | tf_op jit(solution)/shard_map/ppermute | solution.py:499
  382.0 93.3 %collective-permute-start = (bf16[4,160,1792]{2,1,0:T(8,128)(2,1)}, bf16[4,160,1792]{2,1,0:T(8,128)(2,1)}, u32[]{:S(2)}, u32[]{:S(2)}) collective-permute-start(bf16[4,160,1792]{2,1,0:T(8,128)(2,1)} %get-tuple-element.36), channel_id=1, source_target_pairs={{0,4},{1,5},{2,6},{3,7},{4,8},{5,9},{6,10},{7,11},{8,12},{9,13},{1... | collective-permute-start | bytes 6881288 | tf_op jit(solution)/shard_map/ppermute | solution.py:499
  383.6 91.7 %collective-permute-start.1 = (bf16[4,160,1792]{2,1,0:T(8,128)(2,1)}, bf16[4,160,1792]{2,1,0:T(8,128)(2,1)}, u32[]{:S(2)}, u32[]{:S(2)}) collective-permute-start(bf16[4,160,1792]{2,1,0:T(8,128)(2,1)} %get-tuple-element.37), channel_id=1, source_target_pairs={{0,12},{1,13},{2,14},{3,15},{4,0},{5,1},{6,2},{7,3},{8,4},{9,5},{1... | collective-permute-start | bytes 6881288 | tf_op jit(solution)/shard_map/ppermute | solution.py:499
  383.6 94.4 %collective-permute-start.2 = (bf16[4,160,1792]{2,1,0:T(8,128)(2,1)}, bf16[4,160,1792]{2,1,0:T(8,128)(2,1)}, u32[]{:S(2)}, u32[]{:S(2)}) collective-permute-start(bf16[4,160,1792]{2,1,0:T(8,128)(2,1)} %get-tuple-element.38), channel_id=1, source_target_pairs={{0,1},{1,2},{2,3},{3,0},{4,5},{5,6},{6,7},{7,4},{8,9},{9,10},{10,1... | collective-permute-start | bytes 6881288 | tf_op jit(solution)/shard_map/ppermute | solution.py:499
  402.0 70.2 %collective-permute-start.6 = (bf16[3,160,1792]{2,1,0:T(8,128)(2,1)}, bf16[3,160,1792]{2,1,0:T(8,128)(2,1)}, u32[]{:S(2)}, u32[]{:S(2)}) collective-permute-start(bf16[3,160,1792]{2,1,0:T(8,128)(2,1)} %get-tuple-element.42), channel_id=1, source_target_pairs={{0,1},{1,2},{2,3},{3,0},{4,5},{5,6},{6,7},{7,4},{8,9},{9,10},{10,1... | collective-permute-start | bytes 5160968 | tf_op jit(solution)/shard_map/ppermute | solution.py:499
  414.1 58.1 %collective-permute-start.7 = (bf16[3,160,1792]{2,1,0:T(8,128)(2,1)}, bf16[3,160,1792]{2,1,0:T(8,128)(2,1)}, u32[]{:S(2)}, u32[]{:S(2)}) collective-permute-start(bf16[3,160,1792]{2,1,0:T(8,128)(2,1)} %get-tuple-element.43), channel_id=1, source_target_pairs={{0,3},{1,0},{2,1},{3,2},{4,7},{5,4},{6,5},{7,6},{8,11},{9,8},{10,9... | collective-permute-start | bytes 5160968 | tf_op jit(solution)/shard_map/ppermute | solution.py:499
  472.2 175.5 %collective-permute-start.8 = (bf16[160,1792]{1,0:T(8,128)(2,1)}, bf16[160,1792]{1,0:T(8,128)(2,1)}, u32[]{:S(2)}, u32[]{:S(2)}) collective-permute-start(bf16[160,1792]{1,0:T(8,128)(2,1)} %get-tuple-element.63), channel_id=1, source_target_pairs={{0,3},{1,0},{2,1},{3,2},{4,7},{5,4},{6,5},{7,6},{8,11},{9,8},{10,9... | collective-permute-start | bytes 1720328 | tf_op jit(solution)/shard_map/ppermute | solution.py:499
  472.3 175.4 %collective-permute-start.9 = (bf16[160,1792]{1,0:T(8,128)(2,1)}, bf16[160,1792]{1,0:T(8,128)(2,1)}, u32[]{:S(2)}, u32[]{:S(2)}) collective-permute-start(bf16[160,1792]{1,0:T(8,128)(2,1)} %get-tuple-element.64), channel_id=1, source_target_pairs={{0,1},{1,2},{2,3},{3,0},{4,5},{5,6},{6,7},{7,4},{8,9},{9,10},{10,1... | collective-permute-start | bytes 1720328 | tf_op jit(solution)/shard_map/ppermute | solution.py:499
  475.3 172.4 %collective-permute-start.10 = (bf16[160,1792]{1,0:T(8,128)(2,1)}, bf16[160,1792]{1,0:T(8,128)(2,1)}, u32[]{:S(2)}, u32[]{:S(2)}) collective-permute-start(bf16[160,1792]{1,0:T(8,128)(2,1)} %get-tuple-element.65), channel_id=1, source_target_pairs={{0,12},{1,13},{2,14},{3,15},{4,0},{5,1},{6,2},{7,3},{8,4},{9,5},{1... | collective-permute-start | bytes 1720328 | tf_op jit(solution)/shard_map/ppermute | solution.py:499
  475.3 172.4 %collective-permute-start.11 = (bf16[160,1792]{1,0:T(8,128)(2,1)}, bf16[160,1792]{1,0:T(8,128)(2,1)}, u32[]{:S(2)}, u32[]{:S(2)}) collective-permute-start(bf16[160,1792]{1,0:T(8,128)(2,1)} %get-tuple-element.66), channel_id=1, source_target_pairs={{0,4},{1,5},{2,6},{3,7},{4,8},{5,9},{6,10},{7,11},{8,12},{9,13},{1... | collective-permute-start | bytes 1720328 | tf_op jit(solution)/shard_map/ppermute | solution.py:499
  478.0 76.8 %collective-permute-start.3 = (bf16[4,160,1792]{2,1,0:T(8,128)(2,1)}, bf16[4,160,1792]{2,1,0:T(8,128)(2,1)}, u32[]{:S(2)}, u32[]{:S(2)}) collective-permute-start(bf16[4,160,1792]{2,1,0:T(8,128)(2,1)} %get-tuple-element.39), channel_id=1, source_target_pairs={{0,3},{1,0},{2,1},{3,2},{4,7},{5,4},{6,5},{7,6},{8,11},{9,8},{10,9... | collective-permute-start | bytes 6881288 | tf_op jit(solution)/shard_map/ppermute | solution.py:499

commit v4 on v3

--- a/solution.py
+++ b/solution.py
@@ -123,7 +123,7 @@
         self.own, self.every, self.send_sem, self.recv_sem = own, every, send_sem, recv_sem
         self.torus, self.rows = torus, own.shape[0]
         self.unit = self.rows // 4
-        self.sent, self.pending = [], {}
+        self.sent, self.pending = [0] * 4, {}
         for link, (dx, dy) in enumerate(STEPS):
             flat = [p for stage in pieces_of(link) for p in stage]
             for k, (ox, oy, q) in enumerate(flat):
@@ -143,7 +143,7 @@
         return pltpu.make_async_remote_copy(
             src_ref=source,
             dst_ref=target,
-            send_sem=self.send_sem.at[link, k],
+            send_sem=self.send_sem.at[link],
             recv_sem=self.recv_sem.at[link, k],
             device_id={"tp": self.torus.at(*STEPS[link])},
             device_id_type=MESH,
@@ -178,7 +178,7 @@
                 else:
                     before, source = self.arriving(ox, oy, q), place
                 copies.append((before, self.copy(link, k, source, place)))
-                self.sent.append((link, k, place))
+                self.sent[link] += 1
         return copies
 
     def wait_shard(self, ox, oy):
@@ -186,9 +186,11 @@
             self.wait(ox, oy, q)
 
     def finish_sends(self):
-        for link, k, place in self.sent:
-            self.copy(link, k, place, place).wait_send()
-        self.sent.clear()
+        for link, count in enumerate(self.sent):
+            if count:
+                sent = self.every.at[pl.ds(0, count * self.unit)]
+                self.copy(link, 0, sent, sent).wait_send()
+        self.sent = [0] * 4
 
     def finish(self):
         for key in list(self.pending):
@@ -463,7 +465,7 @@
             pltpu.VMEM(block, x.dtype),
             pltpu.VMEM(block, jnp.float32),
             pltpu.VMEM((2, group * rows, tile), x.dtype),
-            *[dma((4, 15))] * 4,
+            *[dma((4,)), dma((4, 15))] * 2,
             dma((4,)),
             dma((5,)),
             dma,
@@ -513,7 +515,7 @@
     relay, direct, later, own_terms = (refs[4 * i : 4 * i + 4] for i in range(4))
     (
         kept_ref, last_ref, later_got, cross_got, later_out, cross_out, exact_in, narrow_in, sums,
-        later_send, later_recv, cross_send, cross_recv, exact_sem, narrow_sem, kept_sem,
+        later_send, later_recv, cross_send, cross_recv, exact_sem, narrow_sem,
     ) = refs[16:]
     rows, quarter = exact_in.shape[1:]
     torus = Torus(side)
@@ -530,7 +532,7 @@
         )
 
     later_copies = {
-        (link, j): remote(link, later_out.at[link, j], later_got.at[link, j], later_send.at[link, j], later_recv.at[link, j])
+        (link, j): remote(link, later_out.at[link, j], later_got.at[link, j], later_send.at[link], later_recv.at[link, j])
         for link in range(4)
         for j in range(side)
     }
@@ -542,7 +544,7 @@
             takes[q][3 if k == 1 else 2],
             cross_out.at[q, k],
             last_ref.at[:, columns[q]] if k == 2 else cross_got.at[q, k],
-            cross_send.at[q, k],
+            cross_send.at[q],
             cross_recv.at[q, k],
         )
         for q in range(4)
@@ -608,16 +610,13 @@
         cross_copies[q, 0].wait_recv()
         add(cross_out.at[q, 2], sums.at[q, 1], cross_got.at[q, 0])
         cross_copies[q, 2].start()
-    outs = []
     for q in range(4):
         cross_copies[q, 1].wait_recv()
-        add(sums.at[q, 1], sums.at[q, 0], cross_got.at[q, 1])
-        outs.append(pltpu.make_async_copy(sums.at[q, 1], kept_ref.at[:, columns[q]], kept_sem.at[q]))
-        outs[-1].start()
-    for c in outs:
-        c.wait()
-    for c in [*later_copies.values(), *cross_copies.values()]:
-        c.wait_send()
+        add(kept_ref.at[:, columns[q]], sums.at[q, 0], cross_got.at[q, 1])
+    for link in range(4):
+        remote(link, later_out.at[link], later_out.at[link], later_send.at[link], later_recv.at[link, 0]).wait_send()
+    for q in range(4):
+        remote(takes[q][2], cross_out.at[q], cross_out.at[q], cross_send.at[q], cross_recv.at[q, 0]).wait_send()
     for q in range(4):
         cross_copies[q, 2].wait_recv()
 
@@ -630,9 +629,9 @@
     piece, slots = (rows, quarter), 4
     return pl.pallas_call(
         functools.partial(scatter_kernel, side),
-        out_shape=[jax.ShapeDtypeStruct((rows, 4 * quarter), t) for t in (jnp.float32, kind)],
+        out_shape=[pltpu.VMEM((rows, 4 * quarter), t) for t in (jnp.float32, kind)],
         in_specs=[any_space] * 16,
-        out_specs=[any_space] * 2,
+        out_specs=[pl.BlockSpec(memory_space=pltpu.VMEM)] * 2,
         scratch_shapes=[
             pltpu.VMEM((4, side, *piece), kind),
             pltpu.VMEM((4, 2, *piece), kind),
@@ -641,16 +640,15 @@
             pltpu.VMEM((slots, *piece), jnp.float32),
             pltpu.VMEM((slots, *piece), kind),
             pltpu.VMEM((4, 2, *piece), jnp.float32),
+            dma((4,)),
             dma((4, side)),
-            dma((4, side)),
-            dma((4, 3)),
+            dma((4,)),
             dma((4, 3)),
             dma((slots,)),
             dma((slots,)),
-            dma((4,)),
         ],
         compiler_params=pltpu.CompilerParams(
-            collective_id=1, has_side_effects=True, vmem_limit_bytes=67_043_328
+            collective_id=1, has_side_effects=True, vmem_limit_bytes=54 * 1024 * 1024
         ),
         cost_estimate=pl.CostEstimate(
             flops=8 * side * rows * quarter, bytes_accessed=60 * side * rows * quarter, transcendentals=0
@@ -660,13 +658,11 @@
 
 
 def finish_kernel(kept_ref, last_ref, *refs):
-    direct, (dx_ref, kept, last, owner, dx, kept_sem, last_sem, owner_sem, dx_sem) = refs[:4], refs[4:]
-    quarter = kept.shape[2]
+    direct, (dx_ref, owner, dx, owner_sem, dx_sem) = refs[:4], refs[4:]
+    quarter = owner.shape[2]
     columns = [pl.ds(q * quarter, quarter) for q in range(4)]
     loads = [
         [
-            pltpu.make_async_copy(kept_ref.at[:, columns[q]], kept.at[q], kept_sem.at[q]),
-            pltpu.make_async_copy(last_ref.at[:, columns[q]], last.at[q], last_sem.at[q]),
             pltpu.make_async_copy(direct[q], owner.at[q], owner_sem.at[q]),
         ]
         for q in range(4)
@@ -678,7 +674,7 @@
     for q, copies in enumerate(loads):
         for c in copies:
             c.wait()
-        total = kept[q] + owner[q].astype(jnp.float32) + last[q].astype(jnp.float32)
+        total = kept_ref[:, columns[q]] + owner[q].astype(jnp.float32) + last_ref[:, columns[q]].astype(jnp.float32)
         dx[q] = total.astype(dx.dtype)
         stores.append(pltpu.make_async_copy(dx.at[q], dx_ref.at[:, columns[q]], dx_sem.at[q]))
         stores[-1].start()
@@ -693,13 +689,11 @@
     any_space = pl.BlockSpec(memory_space=pl.ANY)
     return pl.pallas_call(
         finish_kernel,
-        in_specs=[any_space] * 6,
+        in_specs=[pl.BlockSpec(memory_space=pltpu.VMEM)] * 2 + [any_space] * 4,
         out_specs=any_space,
         out_shape=jax.ShapeDtypeStruct(kept.shape, last.dtype),
-        scratch_shapes=[pltpu.VMEM(pieces, jnp.float32)]
-        + [pltpu.VMEM(pieces, last.dtype)] * 3
-        + [pltpu.SemaphoreType.DMA((4,))] * 4,
-        compiler_params=pltpu.CompilerParams(vmem_limit_bytes=60 * 1024 * 1024),
+        scratch_shapes=[pltpu.VMEM(pieces, last.dtype)] * 2 + [pltpu.SemaphoreType.DMA((4,))] * 2,
+        compiler_params=pltpu.CompilerParams(vmem_limit_bytes=32 * 1024 * 1024),
         cost_estimate=pl.CostEstimate(flops=2 * rows * depth, bytes_accessed=10 * rows * depth, transcendentals=0),
         name="finish_dx",
     )(kept, last, *(direct_last[takes[q][1]] for q in range(4)))

time: 653 us -> 650 us (level)
  no operation moved by 1% of the time
where the time goes in v4:
time: 650 us
  Pallas kernels  550 us (85%)
  waiting for transfers between devices  82.2 us (13%)
  starting transfers between devices  14 us (2%)
    pallas_call x1, Pallas kernels, gather_and_differentiate(): pl.pallas_call(functools.partial(gather_kernel, side), out_shape=[like((g...  379 us
    pallas_call x1, Pallas kernels, sum_and_scatter(): pl.pallas_call(functools.partial(scatter_kernel, side), out_shape=[pltpu....  92.3 us
    ppermute x12, waiting for transfers between devices, shift(): return lax.ppermute(value, ('dp', 'tp'), pairs)  82.2 us
    pallas_call x1, Pallas kernels, dw_in_and_copy(): pl.pallas_call(dw_in_kernel, grid=(steps,), in_specs=[pl.BlockSpec((token...  76.8 us
    ppermute x12, starting transfers between devices, shift(): return lax.ppermute(value, ('dp', 'tp'), pairs)  14 us
  transfers between devices with their start and end apart: 12, of which 3 were waited for; matrix products, arithmetic and copies ran while one was open for 0% of the time, Pallas kernels for 26%

profile of v4, /device:TPU:97, one launch (start us, length us, event | category | flops | bytes accessed | tf_op | source)
XLA Modules:
  0.0 650.0 jit_solution(10446611294967121541)
XLA Ops:
  0.6 378.8 %gather_and_differentiate.1 = (bf16[2560,7168]{1,0:T(8,128)(2,1)}, bf16[2560,7168]{1,0:T(8,128)(2,1)}, bf16[2560,1792]{1,0:T(8,128)(2,1)}, bf16[2560,1792]{1,0:T...) custom-call(bf16[160,7168]{1,0:T(8,128)(2,1)} %x_ref.1, ...), custom_call_target="tpu_custom_call" | custom-call | flops 197300060160 | bytes 370671616 | tf_op jit(solution)/shard_map/gather_and_differentiate/pallas_call | solution.py:447
  379.5 0.5 collective-permute-start.4
  379.9 1.1 collective-permute-start.5
  381.0 1.6 collective-permute-start
  382.6 2.3 collective-permute-start.2
  384.9 16.1 %collective-permute-done.4.refs_4_ = bf16[3,160,1792]{2,1,0:T(8,128)(2,1)S(1)} collective-permute-done((bf16[3,160,1792]{2,1,0:T(8,128)(2,1)}, bf16[3,160,1792]{2,1,0:T(8,128)(2,1)S(1)}, u32[]{:S(2)}, u32[]{:S(2)}) %collective-permute-start.4) | collective-permute-done | bytes 1720352 | tf_op jit(solution)/shard_map/ppermute | solution.py:501
  401.0 0.5 collective-permute-start.6
  401.5 11.7 %collective-permute-done.5.refs_5_ = bf16[3,160,1792]{2,1,0:T(8,128)(2,1)S(1)} collective-permute-done((bf16[3,160,1792]{2,1,0:T(8,128)(2,1)}, bf16[3,160,1792]{2,1,0:T(8,128)(2,1)S(1)}, u32[]{:S(2)}, u32[]{:S(2)}) %collective-permute-start.5) | collective-permute-done | bytes 1720352 | tf_op jit(solution)/shard_map/ppermute | solution.py:501
  413.1 3.6 collective-permute-start.7
  416.7 54.4 %collective-permute-done.6.refs_6_ = bf16[3,160,1792]{2,1,0:T(8,128)(2,1)S(1)} collective-permute-done((bf16[3,160,1792]{2,1,0:T(8,128)(2,1)}, bf16[3,160,1792]{2,1,0:T(8,128)(2,1)S(1)}, u32[]{:S(2)}, u32[]{:S(2)}) %collective-permute-start.6) | collective-permute-done | bytes 1720352 | tf_op jit(solution)/shard_map/ppermute | solution.py:501
  471.2 0.0 collective-permute-done.7.refs_7_
  471.2 3.1 collective-permute-start.9
  474.3 0.0 collective-permute-done.refs_0_
  474.3 0.0 collective-permute-start.10
  474.3 1.4 copy-done
  475.7 1.4 copy-done.1
  477.1 1.3 collective-permute-start.11
  478.4 0.0 collective-permute-done.2.refs_2_
  478.4 0.1 collective-permute-start.3
  478.5 76.8 %shard_map.76 = (bf16[7168,1792]{1,0:T(8,128)(2,1)}, bf16[1792,7168]{1,0:T(8,128)(2,1)}) custom-call(bf16[2560,7168]{1,0:T(8,128)(2,1)} %get-tuple-element.44.x_ref, bf16[2560,1792]{1,0:T(8,128)(2,1)} %get-tuple-element.45.d_pre_ref, bf16[1792,7168]{1,0:T(8,128)(2,1)} %get-tuple-element.46.dw_down_in), custom_call_target="tpu_custom_call" | custom-call | flops 65766686720 | bytes 122945536 | tf_op jit(solution)/shard_map/pallas_call | solution.py:56
  555.3 0.0 collective-permute-done.3.refs_3_
  555.4 92.3 %sum_and_scatter.1 = (f32[160,7168]{1,0:T(8,128)S(1)}, bf16[160,7168]{1,0:T(8,128)(2,1)S(1)}) custom-call(bf16[4,160,1792]{2,1,0:T(8,128)(2,1)} %copy-done, bf16[4,160,1792]{2,1,0:T(8,128)(2,1)} %copy-done.1, bf16[4,160,1792]{2,1,0:T(8,128)(2,1)} %collective-permute-done.2.refs_2_, bf16[4,160,1792]{2,1,0:T(8,128)(2,1)} %collective-permute-done.3.refs_3_, ...), custom_call_target="tpu_custom_call" | custom-call | flops 9175040 | bytes 68812800 | tf_op jit(solution)/shard_map/sum_and_scatter/pallas_call | solution.py:630
  647.7 0.0 collective-permute-done.8.refs_0_
  647.7 2.0 finish_dx.1
  (16 shorter events, 0.0 us)
Async XLA Ops:
  379.5 21.5 %collective-permute-start.4 = (bf16[3,160,1792]{2,1,0:T(8,128)(2,1)}, bf16[3,160,1792]{2,1,0:T(8,128)(2,1)S(1)}, u32[]{:S(2)}, u32[]{:S(2)}) collective-permute-start(bf16[3,160,1792]{2,1,0:T(8,128)(2,1)} %get-tuple-element.40), channel_id=1, source_target_pairs={{0,4},{1,5},{2,6},{3,7},{4,8},{5,9},{6,10},{7,11},{8,12},{9,13},{1... | collective-permute-start | bytes 5160968 | tf_op jit(solution)/shard_map/ppermute | solution.py:501
  379.9 33.2 %collective-permute-start.5 = (bf16[3,160,1792]{2,1,0:T(8,128)(2,1)}, bf16[3,160,1792]{2,1,0:T(8,128)(2,1)S(1)}, u32[]{:S(2)}, u32[]{:S(2)}) collective-permute-start(bf16[3,160,1792]{2,1,0:T(8,128)(2,1)} %get-tuple-element.41), channel_id=1, source_target_pairs={{0,12},{1,13},{2,14},{3,15},{4,0},{5,1},{6,2},{7,3},{8,4},{9,5},{1... | collective-permute-start | bytes 5160968 | tf_op jit(solution)/shard_map/ppermute | solution.py:501
  381.0 93.3 %collective-permute-start = (bf16[4,160,1792]{2,1,0:T(8,128)(2,1)}, bf16[4,160,1792]{2,1,0:T(8,128)(2,1)S(1)}, u32[]{:S(2)}, u32[]{:S(2)}) collective-permute-start(bf16[4,160,1792]{2,1,0:T(8,128)(2,1)} %get-tuple-element.36), channel_id=1, source_target_pairs={{0,4},{1,5},{2,6},{3,7},{4,8},{5,9},{6,10},{7,11},{8,12},{9,13},{1... | collective-permute-start | bytes 6881288 | tf_op jit(solution)/shard_map/ppermute | solution.py:501
  382.6 91.7 %collective-permute-start.1 = (bf16[4,160,1792]{2,1,0:T(8,128)(2,1)}, bf16[4,160,1792]{2,1,0:T(8,128)(2,1)S(1)}, u32[]{:S(2)}, u32[]{:S(2)}) collective-permute-start(bf16[4,160,1792]{2,1,0:T(8,128)(2,1)} %get-tuple-element.37), channel_id=1, source_target_pairs={{0,12},{1,13},{2,14},{3,15},{4,0},{5,1},{6,2},{7,3},{8,4},{9,5},{1... | collective-permute-start | bytes 6881288 | tf_op jit(solution)/shard_map/ppermute | solution.py:501
  382.6 95.7 %collective-permute-start.2 = (bf16[4,160,1792]{2,1,0:T(8,128)(2,1)}, bf16[4,160,1792]{2,1,0:T(8,128)(2,1)}, u32[]{:S(2)}, u32[]{:S(2)}) collective-permute-start(bf16[4,160,1792]{2,1,0:T(8,128)(2,1)} %get-tuple-element.38), channel_id=1, source_target_pairs={{0,1},{1,2},{2,3},{3,0},{4,5},{5,6},{6,7},{7,4},{8,9},{9,10},{10,1... | collective-permute-start | bytes 6881288 | tf_op jit(solution)/shard_map/ppermute | solution.py:501
  401.0 77.4 %copy-start.2 = (bf16[3,160,1792]{2,1,0:T(8,128)(2,1)}, bf16[3,160,1792]{2,1,0:T(8,128)(2,1)S(1)}, u32[]{:S(2)}) copy-start(bf16[3,160,1792]{2,1,0:T(8,128)(2,1)S(1)} %collective-permute-done.4.refs_4_) | copy-start | bytes 5160964
  401.0 70.2 %collective-permute-start.6 = (bf16[3,160,1792]{2,1,0:T(8,128)(2,1)}, bf16[3,160,1792]{2,1,0:T(8,128)(2,1)S(1)}, u32[]{:S(2)}, u32[]{:S(2)}) collective-permute-start(bf16[3,160,1792]{2,1,0:T(8,128)(2,1)} %get-tuple-element.42), channel_id=1, source_target_pairs={{0,1},{1,2},{2,3},{3,0},{4,5},{5,6},{6,7},{7,4},{8,9},{9,10},{10,1... | collective-permute-start | bytes 5160968 | tf_op jit(solution)/shard_map/ppermute | solution.py:501
  413.1 65.2 %copy-start.3 = (bf16[3,160,1792]{2,1,0:T(8,128)(2,1)}, bf16[3,160,1792]{2,1,0:T(8,128)(2,1)S(1)}, u32[]{:S(2)}) copy-start(bf16[3,160,1792]{2,1,0:T(8,128)(2,1)S(1)} %collective-permute-done.5.refs_5_) | copy-start | bytes 5160964
  413.1 58.1 %collective-permute-start.7 = (bf16[3,160,1792]{2,1,0:T(8,128)(2,1)}, bf16[3,160,1792]{2,1,0:T(8,128)(2,1)S(1)}, u32[]{:S(2)}, u32[]{:S(2)}) collective-permute-start(bf16[3,160,1792]{2,1,0:T(8,128)(2,1)} %get-tuple-element.43), channel_id=1, source_target_pairs={{0,3},{1,0},{2,1},{3,2},{4,7},{5,4},{6,5},{7,6},{8,11},{9,8},{10,9... | collective-permute-start | bytes 5160968 | tf_op jit(solution)/shard_map/ppermute | solution.py:501
  471.2 7.2 %copy-start.4 = (bf16[3,160,1792]{2,1,0:T(8,128)(2,1)}, bf16[3,160,1792]{2,1,0:T(8,128)(2,1)S(1)}, u32[]{:S(2)}) copy-start(bf16[3,160,1792]{2,1,0:T(8,128)(2,1)S(1)} %collective-permute-done.6.refs_6_) | copy-start | bytes 5160964
  471.2 176.5 %collective-permute-start.8 = (bf16[160,1792]{1,0:T(8,128)(2,1)}, bf16[160,1792]{1,0:T(8,128)(2,1)S(1)}, u32[]{:S(2)}, u32[]{:S(2)}) collective-permute-start(bf16[160,1792]{1,0:T(8,128)(2,1)} %get-tuple-element.63), channel_id=1, source_target_pairs={{0,3},{1,0},{2,1},{3,2},{4,7},{5,4},{6,5},{7,6},{8,11},{9,8},{10,9... | collective-permute-start | bytes 1720328 | tf_op jit(solution)/shard_map/ppermute | solution.py:501
  471.2 7.3 %copy-start.5 = (bf16[3,160,1792]{2,1,0:T(8,128)(2,1)}, bf16[3,160,1792]{2,1,0:T(8,128)(2,1)S(1)}, u32[]{:S(2)}) copy-start(bf16[3,160,1792]{2,1,0:T(8,128)(2,1)S(1)} %collective-permute-done.7.refs_7_) | copy-start | bytes 5160964
  471.2 176.5 %collective-permute-start.9 = (bf16[160,1792]{1,0:T(8,128)(2,1)}, bf16[160,1792]{1,0:T(8,128)(2,1)S(1)}, u32[]{:S(2)}, u32[]{:S(2)}) collective-permute-start(bf16[160,1792]{1,0:T(8,128)(2,1)} %get-tuple-element.64), channel_id=1, source_target_pairs={{0,1},{1,2},{2,3},{3,0},{4,5},{5,6},{6,7},{7,4},{8,9},{9,10},{10,1... | collective-permute-start | bytes 1720328 | tf_op jit(solution)/shard_map/ppermute | solution.py:501
  474.3 1.4 copy-start
  474.3 173.4 %collective-permute-start.10 = (bf16[160,1792]{1,0:T(8,128)(2,1)}, bf16[160,1792]{1,0:T(8,128)(2,1)S(1)}, u32[]{:S(2)}, u32[]{:S(2)}) collective-permute-start(bf16[160,1792]{1,0:T(8,128)(2,1)} %get-tuple-element.65), channel_id=1, source_target_pairs={{0,12},{1,13},{2,14},{3,15},{4,0},{5,1},{6,2},{7,3},{8,4},{9,5},{1... | collective-permute-start | bytes 1720328 | tf_op jit(solution)/shard_map/ppermute | solution.py:501
  475.7 1.4 copy-start.1
  477.1 170.7 %collective-permute-start.11 = (bf16[160,1792]{1,0:T(8,128)(2,1)}, bf16[160,1792]{1,0:T(8,128)(2,1)S(1)}, u32[]{:S(2)}, u32[]{:S(2)}) collective-permute-start(bf16[160,1792]{1,0:T(8,128)(2,1)} %get-tuple-element.66), channel_id=1, source_target_pairs={{0,4},{1,5},{2,6},{3,7},{4,8},{5,9},{6,10},{7,11},{8,12},{9,13},{1... | collective-permute-start | bytes 1720328 | tf_op jit(solution)/shard_map/ppermute | solution.py:501
  478.4 77.0 %collective-permute-start.3 = (bf16[4,160,1792]{2,1,0:T(8,128)(2,1)}, bf16[4,160,1792]{2,1,0:T(8,128)(2,1)}, u32[]{:S(2)}, u32[]{:S(2)}) collective-permute-start(bf16[4,160,1792]{2,1,0:T(8,128)(2,1)} %get-tuple-element.39), channel_id=1, source_target_pairs={{0,3},{1,0},{2,1},{3,2},{4,7},{5,4},{6,5},{7,6},{8,11},{9,8},{10,9... | collective-permute-start | bytes 6881288 | tf_op jit(solution)/shard_map/ppermute | solution.py:501

commit v5 on v4

--- a/solution.py
+++ b/solution.py
@@ -118,8 +118,14 @@
     )
 
 
+TOGETHER = (0, 1), (2, 3), (4,), (5, 6, 7, 8), (9, 10), (11, 12, 13, 14)
+APART = *TOGETHER[:-1], (11,), (12,), (13,), (14,)
+
+
 class Gather:
-    def __init__(self, own, every, send_sem, recv_sem, torus):
+    def __init__(self, own, every, send_sem, recv_sem, torus, groups):
+        self.groups = groups
+        self.group_of = {k: g for g, pieces in enumerate(groups) for k in pieces}
         self.own, self.every, self.send_sem, self.recv_sem = own, every, send_sem, recv_sem
         self.torus, self.rows = torus, own.shape[0]
         self.unit = self.rows // 4
@@ -130,7 +136,6 @@
                 key = self.key(ox - dx, oy - dy, q)
                 assert key not in self.pending
                 self.pending[key] = (link, k)
-        self.arrival = dict(self.pending)
 
     def key(self, ox, oy, q):
         return ox % self.torus.side, oy % self.torus.side, q
@@ -144,15 +149,19 @@
             src_ref=source,
             dst_ref=target,
             send_sem=self.send_sem.at[link],
-            recv_sem=self.recv_sem.at[link, k],
+            recv_sem=self.recv_sem.at[link, self.group_of[k]],
             device_id={"tp": self.torus.at(*STEPS[link])},
             device_id_type=MESH,
         )
 
     def arriving(self, ox, oy, q):
-        found = self.pending.pop(self.key(ox, oy, q), None)
-        place = self.place(ox, oy, q)
-        return [] if found is None else [self.copy(*found, place, place)]
+        if self.key(ox, oy, q) not in self.pending:
+            return []
+        link, k = self.pending[self.key(ox, oy, q)]
+        group = self.groups[self.group_of[k]]
+        self.pending = {key: (l, p) for key, (l, p) in self.pending.items() if l != link or p not in group}
+        arrived = self.every.at[pl.ds(0, len(group) * self.unit)]
+        return [self.copy(link, k, arrived, arrived)]
 
     def wait(self, ox, oy, q):
         for c in self.arriving(ox, oy, q):
@@ -236,8 +245,8 @@
     torus = Torus(side)
     barrier_with_neighbours(torus)
 
-    dys = Gather(dy_ref, dy_all, dy_send, dy_recv, torus)
-    xs = Gather(x_ref, x_all, x_send, x_recv, torus)
+    dys = Gather(dy_ref, dy_all, dy_send, dy_recv, torus, APART)
+    xs = Gather(x_ref, x_all, x_send, x_recv, torus, TOGETHER)
     dys.send(0)
 
     def load_quarter(q):
@@ -465,7 +474,10 @@
             pltpu.VMEM(block, x.dtype),
             pltpu.VMEM(block, jnp.float32),
             pltpu.VMEM((2, group * rows, tile), x.dtype),
-            *[dma((4,)), dma((4, 15))] * 2,
+            dma((4,)),
+            dma((4, len(TOGETHER))),
+            dma((4,)),
+            dma((4, len(APART))),
             dma((4,)),
             dma((5,)),
             dma,

time: 650 us -> 650 us (level)
  no operation moved by 1% of the time
where the time goes in v5:
time: 650 us; the launch traced here: 649 us
  Pallas kernels  549 us (84%)
  waiting for transfers between devices  81.6 us (13%)
  starting transfers between devices  14.6 us (2%)
    pallas_call x1, Pallas kernels, gather_and_differentiate(): pl.pallas_call(functools.partial(gather_kernel, side), out_shape=[like((g...  378 us
    pallas_call x1, Pallas kernels, sum_and_scatter(): pl.pallas_call(functools.partial(scatter_kernel, side), out_shape=[pltpu....  92.6 us
    ppermute x12, waiting for transfers between devices, shift(): return lax.ppermute(value, ('dp', 'tp'), pairs)  81.6 us
    pallas_call x1, Pallas kernels, dw_in_and_copy(): pl.pallas_call(dw_in_kernel, grid=(steps,), in_specs=[pl.BlockSpec((token...  76.6 us
    ppermute x12, starting transfers between devices, shift(): return lax.ppermute(value, ('dp', 'tp'), pairs)  14.6 us
  transfers between devices with their start and end apart: 12, of which 3 were waited for; matrix products, arithmetic and copies ran while one was open for 0% of the time, Pallas kernels for 26%

profile of v5, /device:TPU:97, one launch (start us, length us, event | category | flops | bytes accessed | tf_op | source)
XLA Modules:
  0.0 649.4 jit_solution(2561638472613983458)
XLA Ops:
  0.6 378.3 %gather_and_differentiate.1 = (bf16[2560,7168]{1,0:T(8,128)(2,1)}, bf16[2560,7168]{1,0:T(8,128)(2,1)}, bf16[2560,1792]{1,0:T(8,128)(2,1)}, bf16[2560,1792]{1,0:T...) custom-call(bf16[160,7168]{1,0:T(8,128)(2,1)} %x_ref.1, ...), custom_call_target="tpu_custom_call" | custom-call | flops 197300060160 | bytes 370671616 | tf_op jit(solution)/shard_map/gather_and_differentiate/pallas_call | solution.py:456
  378.9 0.1 collective-permute-start.4
  379.0 1.4 collective-permute-start.5
  380.5 1.3 collective-permute-start
  381.8 0.1 collective-permute-start.1
  381.9 2.4 collective-permute-start.2
  384.4 16.1 %collective-permute-done.4.refs_4_ = bf16[3,160,1792]{2,1,0:T(8,128)(2,1)S(1)} collective-permute-done((bf16[3,160,1792]{2,1,0:T(8,128)(2,1)}, bf16[3,160,1792]{2,1,0:T(8,128)(2,1)S(1)}, u32[]{:S(2)}, u32[]{:S(2)}) %collective-permute-start.4) | collective-permute-done | bytes 1720352 | tf_op jit(solution)/shard_map/ppermute | solution.py:513
  400.4 0.5 collective-permute-start.6
  400.9 11.1 %collective-permute-done.5.refs_5_ = bf16[3,160,1792]{2,1,0:T(8,128)(2,1)S(1)} collective-permute-done((bf16[3,160,1792]{2,1,0:T(8,128)(2,1)}, bf16[3,160,1792]{2,1,0:T(8,128)(2,1)S(1)}, u32[]{:S(2)}, u32[]{:S(2)}) %collective-permute-start.5) | collective-permute-done | bytes 1720352 | tf_op jit(solution)/shard_map/ppermute | solution.py:513
  412.0 4.2 collective-permute-start.7
  416.2 54.4 %collective-permute-done.6.refs_6_ = bf16[3,160,1792]{2,1,0:T(8,128)(2,1)S(1)} collective-permute-done((bf16[3,160,1792]{2,1,0:T(8,128)(2,1)}, bf16[3,160,1792]{2,1,0:T(8,128)(2,1)S(1)}, u32[]{:S(2)}, u32[]{:S(2)}) %collective-permute-start.6) | collective-permute-done | bytes 1720352 | tf_op jit(solution)/shard_map/ppermute | solution.py:513
  470.6 0.0 collective-permute-start.8
  470.6 3.1 collective-permute-start.9
  473.8 0.0 collective-permute-done.1.refs_1_
  473.8 1.4 copy-done
  475.1 1.4 copy-done.1
  476.5 1.3 collective-permute-start.11
  477.8 0.1 collective-permute-start.3
  478.0 76.6 %shard_map.76 = (bf16[7168,1792]{1,0:T(8,128)(2,1)}, bf16[1792,7168]{1,0:T(8,128)(2,1)}) custom-call(bf16[2560,7168]{1,0:T(8,128)(2,1)} %get-tuple-element.44.x_ref, bf16[2560,1792]{1,0:T(8,128)(2,1)} %get-tuple-element.45.d_pre_ref, bf16[1792,7168]{1,0:T(8,128)(2,1)} %get-tuple-element.46.dw_down_in), custom_call_target="tpu_custom_call" | custom-call | flops 65766686720 | bytes 122945536 | tf_op jit(solution)/shard_map/pallas_call | solution.py:56
  554.5 0.0 collective-permute-done.3.refs_3_
  554.5 92.6 %sum_and_scatter.1 = (f32[160,7168]{1,0:T(8,128)S(1)}, bf16[160,7168]{1,0:T(8,128)(2,1)S(1)}) custom-call(bf16[4,160,1792]{2,1,0:T(8,128)(2,1)} %copy-done, bf16[4,160,1792]{2,1,0:T(8,128)(2,1)} %copy-done.1, bf16[4,160,1792]{2,1,0:T(8,128)(2,1)} %collective-permute-done.2.refs_2_, bf16[4,160,1792]{2,1,0:T(8,128)(2,1)} %collective-permute-done.3.refs_3_, ...), custom_call_target="tpu_custom_call" | custom-call | flops 9175040 | bytes 68812800 | tf_op jit(solution)/shard_map/sum_and_scatter/pallas_call | solution.py:642
  647.2 0.0 collective-permute-done.9.refs_1_
  647.2 0.0 collective-permute-done.10.refs_2_
  647.2 2.0 finish_dx.1
  (16 shorter events, 0.0 us)
Async XLA Ops:
  378.9 21.5 %collective-permute-start.4 = (bf16[3,160,1792]{2,1,0:T(8,128)(2,1)}, bf16[3,160,1792]{2,1,0:T(8,128)(2,1)S(1)}, u32[]{:S(2)}, u32[]{:S(2)}) collective-permute-start(bf16[3,160,1792]{2,1,0:T(8,128)(2,1)} %get-tuple-element.40), channel_id=1, source_target_pairs={{0,4},{1,5},{2,6},{3,7},{4,8},{5,9},{6,10},{7,11},{8,12},{9,13},{1... | collective-permute-start | bytes 5160968 | tf_op jit(solution)/shard_map/ppermute | solution.py:513
  379.0 33.0 %collective-permute-start.5 = (bf16[3,160,1792]{2,1,0:T(8,128)(2,1)}, bf16[3,160,1792]{2,1,0:T(8,128)(2,1)S(1)}, u32[]{:S(2)}, u32[]{:S(2)}) collective-permute-start(bf16[3,160,1792]{2,1,0:T(8,128)(2,1)} %get-tuple-element.41), channel_id=1, source_target_pairs={{0,12},{1,13},{2,14},{3,15},{4,0},{5,1},{6,2},{7,3},{8,4},{9,5},{1... | collective-permute-start | bytes 5160968 | tf_op jit(solution)/shard_map/ppermute | solution.py:513
  380.5 93.3 %collective-permute-start = (bf16[4,160,1792]{2,1,0:T(8,128)(2,1)}, bf16[4,160,1792]{2,1,0:T(8,128)(2,1)S(1)}, u32[]{:S(2)}, u32[]{:S(2)}) collective-permute-start(bf16[4,160,1792]{2,1,0:T(8,128)(2,1)} %get-tuple-element.36), channel_id=1, source_target_pairs={{0,4},{1,5},{2,6},{3,7},{4,8},{5,9},{6,10},{7,11},{8,12},{9,13},{1... | collective-permute-start | bytes 6881288 | tf_op jit(solution)/shard_map/ppermute | solution.py:513
  381.8 92.0 %collective-permute-start.1 = (bf16[4,160,1792]{2,1,0:T(8,128)(2,1)}, bf16[4,160,1792]{2,1,0:T(8,128)(2,1)S(1)}, u32[]{:S(2)}, u32[]{:S(2)}) collective-permute-start(bf16[4,160,1792]{2,1,0:T(8,128)(2,1)} %get-tuple-element.37), channel_id=1, source_target_pairs={{0,12},{1,13},{2,14},{3,15},{4,0},{5,1},{6,2},{7,3},{8,4},{9,5},{1... | collective-permute-start | bytes 6881288 | tf_op jit(solution)/shard_map/ppermute | solution.py:513
  381.9 95.9 %collective-permute-start.2 = (bf16[4,160,1792]{2,1,0:T(8,128)(2,1)}, bf16[4,160,1792]{2,1,0:T(8,128)(2,1)}, u32[]{:S(2)}, u32[]{:S(2)}) collective-permute-start(bf16[4,160,1792]{2,1,0:T(8,128)(2,1)} %get-tuple-element.38), channel_id=1, source_target_pairs={{0,1},{1,2},{2,3},{3,0},{4,5},{5,6},{6,7},{7,4},{8,9},{9,10},{10,1... | collective-permute-start | bytes 6881288 | tf_op jit(solution)/shard_map/ppermute | solution.py:513
  400.4 77.4 %copy-start.2 = (bf16[3,160,1792]{2,1,0:T(8,128)(2,1)}, bf16[3,160,1792]{2,1,0:T(8,128)(2,1)S(1)}, u32[]{:S(2)}) copy-start(bf16[3,160,1792]{2,1,0:T(8,128)(2,1)S(1)} %collective-permute-done.4.refs_4_) | copy-start | bytes 5160964
  400.4 70.2 %collective-permute-start.6 = (bf16[3,160,1792]{2,1,0:T(8,128)(2,1)}, bf16[3,160,1792]{2,1,0:T(8,128)(2,1)S(1)}, u32[]{:S(2)}, u32[]{:S(2)}) collective-permute-start(bf16[3,160,1792]{2,1,0:T(8,128)(2,1)} %get-tuple-element.42), channel_id=1, source_target_pairs={{0,1},{1,2},{2,3},{3,0},{4,5},{5,6},{6,7},{7,4},{8,9},{9,10},{10,1... | collective-permute-start | bytes 5160968 | tf_op jit(solution)/shard_map/ppermute | solution.py:513
  412.0 65.8 %copy-start.3 = (bf16[3,160,1792]{2,1,0:T(8,128)(2,1)}, bf16[3,160,1792]{2,1,0:T(8,128)(2,1)S(1)}, u32[]{:S(2)}) copy-start(bf16[3,160,1792]{2,1,0:T(8,128)(2,1)S(1)} %collective-permute-done.5.refs_5_) | copy-start | bytes 5160964
  412.0 58.6 %collective-permute-start.7 = (bf16[3,160,1792]{2,1,0:T(8,128)(2,1)}, bf16[3,160,1792]{2,1,0:T(8,128)(2,1)S(1)}, u32[]{:S(2)}, u32[]{:S(2)}) collective-permute-start(bf16[3,160,1792]{2,1,0:T(8,128)(2,1)} %get-tuple-element.43), channel_id=1, source_target_pairs={{0,3},{1,0},{2,1},{3,2},{4,7},{5,4},{6,5},{7,6},{8,11},{9,8},{10,9... | collective-permute-start | bytes 5160968 | tf_op jit(solution)/shard_map/ppermute | solution.py:513
  470.6 7.2 %copy-start.4 = (bf16[3,160,1792]{2,1,0:T(8,128)(2,1)}, bf16[3,160,1792]{2,1,0:T(8,128)(2,1)S(1)}, u32[]{:S(2)}) copy-start(bf16[3,160,1792]{2,1,0:T(8,128)(2,1)S(1)} %collective-permute-done.6.refs_6_) | copy-start | bytes 5160964
  470.6 176.5 %collective-permute-start.8 = (bf16[160,1792]{1,0:T(8,128)(2,1)}, bf16[160,1792]{1,0:T(8,128)(2,1)S(1)}, u32[]{:S(2)}, u32[]{:S(2)}) collective-permute-start(bf16[160,1792]{1,0:T(8,128)(2,1)} %get-tuple-element.63), channel_id=1, source_target_pairs={{0,3},{1,0},{2,1},{3,2},{4,7},{5,4},{6,5},{7,6},{8,11},{9,8},{10,9... | collective-permute-start | bytes 1720328 | tf_op jit(solution)/shard_map/ppermute | solution.py:513
  470.6 7.3 %copy-start.5 = (bf16[3,160,1792]{2,1,0:T(8,128)(2,1)}, bf16[3,160,1792]{2,1,0:T(8,128)(2,1)S(1)}, u32[]{:S(2)}) copy-start(bf16[3,160,1792]{2,1,0:T(8,128)(2,1)S(1)} %collective-permute-done.7.refs_7_) | copy-start | bytes 5160964
  470.6 176.5 %collective-permute-start.9 = (bf16[160,1792]{1,0:T(8,128)(2,1)}, bf16[160,1792]{1,0:T(8,128)(2,1)S(1)}, u32[]{:S(2)}, u32[]{:S(2)}) collective-permute-start(bf16[160,1792]{1,0:T(8,128)(2,1)} %get-tuple-element.64), channel_id=1, source_target_pairs={{0,1},{1,2},{2,3},{3,0},{4,5},{5,6},{6,7},{7,4},{8,9},{9,10},{10,1... | collective-permute-start | bytes 1720328 | tf_op jit(solution)/shard_map/ppermute | solution.py:513
  473.8 1.4 copy-start
  473.8 173.4 %collective-permute-start.10 = (bf16[160,1792]{1,0:T(8,128)(2,1)}, bf16[160,1792]{1,0:T(8,128)(2,1)S(1)}, u32[]{:S(2)}, u32[]{:S(2)}) collective-permute-start(bf16[160,1792]{1,0:T(8,128)(2,1)} %get-tuple-element.65), channel_id=1, source_target_pairs={{0,12},{1,13},{2,14},{3,15},{4,0},{5,1},{6,2},{7,3},{8,4},{9,5},{1... | collective-permute-start | bytes 1720328 | tf_op jit(solution)/shard_map/ppermute | solution.py:513
  475.1 1.4 copy-start.1
  476.5 170.7 %collective-permute-start.11 = (bf16[160,1792]{1,0:T(8,128)(2,1)}, bf16[160,1792]{1,0:T(8,128)(2,1)S(1)}, u32[]{:S(2)}, u32[]{:S(2)}) collective-permute-start(bf16[160,1792]{1,0:T(8,128)(2,1)} %get-tuple-element.66), channel_id=1, source_target_pairs={{0,4},{1,5},{2,6},{3,7},{4,8},{5,9},{6,10},{7,11},{8,12},{9,13},{1... | collective-permute-start | bytes 1720328 | tf_op jit(solution)/shard_map/ppermute | solution.py:513
  477.8 76.7 %collective-permute-start.3 = (bf16[4,160,1792]{2,1,0:T(8,128)(2,1)}, bf16[4,160,1792]{2,1,0:T(8,128)(2,1)}, u32[]{:S(2)}, u32[]{:S(2)}) collective-permute-start(bf16[4,160,1792]{2,1,0:T(8,128)(2,1)} %get-tuple-element.39), channel_id=1, source_target_pairs={{0,3},{1,0},{2,1},{3,2},{4,7},{5,4},{6,5},{7,6},{8,11},{9,8},{10,9... | collective-permute-start | bytes 6881288 | tf_op jit(solution)/shard_map/ppermute | solution.py:513
